TPU v7x, 256 devices: a 2x2x32 block of a 4x8x32 slice. The times are simulated.
256 devices in a mesh: branch: 4 (over x, y), seq: 64 (over z, core).
Axes of the slice: x: 2, y: 2, z: 32, core: 2. Of those that a mesh axis runs over, the one named last changes fastest.
The devices are a block of a 4x8x32 slice.
Arguments:
- queries: bfloat16 [65536, 2048], P(('branch', 'seq')), parts along dimension 0, may hold values from -8 to 8
- keys: bfloat16 [65536, 2048], P(('branch', 'seq')), parts along dimension 0, may hold values from -8 to 8
- values: bfloat16 [65536, 2048], P(('branch', 'seq')), parts along dimension 0, may hold values from -6 to 6
- out_grad: bfloat16 [65536, 2048], P(('branch', 'seq')), parts along dimension 0, may hold values from -6 to 6
- segments: int32 [65536], P(('branch', 'seq')), parts along dimension 0, may hold values from 0 to 28, never falling along the last dimension, each value on 1 to 768 neighbouring positions
Outputs:
- attended: bfloat16 [65536, 2048], P(('branch', 'seq')), parts along dimension 0
- query_grad: bfloat16 [65536, 2048], P(('branch', 'seq')), parts along dimension 0
- key_grad: bfloat16 [65536, 2048], P(('branch', 'seq')), parts along dimension 0
- value_grad: bfloat16 [65536, 2048], P(('branch', 'seq')), parts along dimension 0
There are 4 independent parts, one for each index of `branch`. A program takes and returns all parts, laid end to end along the dimension named above; each array names one. Nothing has to cross between parts.
Inputs may be any that keep to these rules, and one draw needn't show every extreme that they name: `segments`: never falling along the sequence; each document has 1 to 768 tokens, and one has exactly 768.
All inputs are finite; a program needn't handle non-finite values.
Results may differ from a plain program's by a relative error of at most 0.017.
Values may be sent and summed in bfloat16 or wider, within the bound.
A program may use at most 128 MiB of HBM per device.

v0:
```python
import math

import jax
import jax.numpy as jnp
from jax import lax
from jax.sharding import PartitionSpec as P

HEADS = 16
REACH = 3


def shifted(x, axis, by):
    peers = lax.axis_size(axis)
    pairs = [(i, i + by) for i in range(peers) if 0 <= i + by < peers]
    return lax.ppermute(x, axis, pairs)


def local(queries, keys, values, out_grad, segments):
    tok_rows = queries.shape[0]
    feature = queries.shape[1]
    head_dim = feature // HEADS
    inv_root = 1.0 / math.sqrt(head_dim)
    dev_index = lax.axis_index("seq")
    dev_count = lax.axis_size("seq")
    query3 = queries.reshape(tok_rows, HEADS, head_dim)
    grad3 = out_grad.reshape(tok_rows, HEADS, head_dim)
    own_block = (keys, values, segments)
    received = [own_block]
    moving = own_block
    for distance in range(1, REACH + 1):
        moving = shifted((moving[0], moving[1], moving[2]), "seq", 1)
        received.append(moving)
    ordered = received[::-1]
    key_all = jnp.concatenate([item[0] for item in ordered], 0).reshape(-1, HEADS, head_dim)
    value_all = jnp.concatenate([item[1] for item in ordered], 0).reshape(-1, HEADS, head_dim)
    key_seg = jnp.concatenate([item[2] for item in ordered], 0)
    key_width = key_all.shape[0]
    query_pos = dev_index * tok_rows + jnp.arange(tok_rows, dtype=jnp.int32)
    key_pos = (dev_index - REACH) * tok_rows + jnp.arange(key_width, dtype=jnp.int32)
    visible = (
        (key_pos[None, :] >= 0)
        & (key_pos[None, :] <= query_pos[:, None])
        & (key_seg[None, :] == segments[:, None])
    )
    scores = (
        jnp.einsum("ihd,jhd->hij", query3, key_all, preferred_element_type=jnp.float32) * inv_root
    )
    scores = jnp.where(visible[None], scores, -jnp.inf)
    row_peak = jnp.max(scores, -1, keepdims=True)
    exponent = jnp.exp(scores - row_peak)
    row_total = jnp.sum(exponent, -1, keepdims=True)
    weights = (exponent / row_total).astype(jnp.bfloat16)
    attended = jnp.einsum(
        "hij,jhd->ihd", weights, value_all, preferred_element_type=jnp.float32
    ).astype(jnp.bfloat16)
    row_delta = jnp.sum(grad3.astype(jnp.float32) * attended.astype(jnp.float32), -1).T
    dprob = jnp.einsum("ihd,jhd->hij", grad3, value_all, preferred_element_type=jnp.float32)
    dscore = (weights.astype(jnp.float32) * (dprob - row_delta[:, :, None]) * inv_root).astype(
        jnp.bfloat16
    )
    query_grad = jnp.einsum(
        "hij,jhd->ihd", dscore, key_all, preferred_element_type=jnp.float32
    ).astype(jnp.bfloat16)
    own_start = REACH * tok_rows
    key_grad = jnp.einsum(
        "hij,ihd->jhd", dscore[:, :, own_start:], query3, preferred_element_type=jnp.float32
    ).reshape(tok_rows, feature)
    value_grad = jnp.einsum(
        "hij,ihd->jhd", weights[:, :, own_start:], grad3, preferred_element_type=jnp.float32
    ).reshape(tok_rows, feature)
    own_keys = key_all[own_start:]
    own_values = value_all[own_start:]
    row_stats = (row_peak[:, :, 0], row_total[:, :, 0], row_delta)
    for distance in range(1, REACH + 1):
        far_query, far_grad, far_seg = shifted((queries, out_grad, segments), "seq", -distance)
        far_peak, far_total, far_delta = shifted(
            (row_stats[0], row_stats[1], row_stats[2]), "seq", -distance
        )
        far_pos = (dev_index + distance) * tok_rows + jnp.arange(tok_rows, dtype=jnp.int32)
        live_rows = far_pos < dev_count * tok_rows
        far_visible = live_rows[:, None] & (far_seg[:, None] == segments[None, :])
        far_query3 = far_query.reshape(tok_rows, HEADS, head_dim)
        far_grad3 = far_grad.reshape(tok_rows, HEADS, head_dim)
        far_scores = (
            jnp.einsum("ihd,jhd->hij", far_query3, own_keys, preferred_element_type=jnp.float32)
            * inv_root
        )
        far_scores = jnp.where(far_visible[None], far_scores, -jnp.inf)
        safe_total = jnp.where(live_rows[None, :], far_total, 1.0)
        safe_peak = jnp.where(live_rows[None, :], far_peak, 0.0)
        far_weights = (jnp.exp(far_scores - safe_peak[:, :, None]) / safe_total[:, :, None]).astype(
            jnp.bfloat16
        )
        far_dprob = jnp.einsum(
            "ihd,jhd->hij", far_grad3, own_values, preferred_element_type=jnp.float32
        )
        far_dscore = (
            far_weights.astype(jnp.float32) * (far_dprob - far_delta[:, :, None]) * inv_root
        ).astype(jnp.bfloat16)
        key_grad = key_grad + jnp.einsum(
            "hij,ihd->jhd", far_dscore, far_query3, preferred_element_type=jnp.float32
        ).reshape(tok_rows, feature)
        value_grad = value_grad + jnp.einsum(
            "hij,ihd->jhd", far_weights, far_grad3, preferred_element_type=jnp.float32
        ).reshape(tok_rows, feature)
    return (
        attended.reshape(tok_rows, feature),
        query_grad.reshape(tok_rows, feature),
        key_grad.astype(jnp.bfloat16),
        value_grad.astype(jnp.bfloat16),
    )


def solution(mesh):
    in_specs = (
        P(("branch", "seq"), None),
        P(("branch", "seq"), None),
        P(("branch", "seq"), None),
        P(("branch", "seq"), None),
        P(("branch", "seq")),
    )
    out_specs = (
        P(("branch", "seq"), None),
        P(("branch", "seq"), None),
        P(("branch", "seq"), None),
        P(("branch", "seq"), None),
    )
    return jax.shard_map(local, mesh=mesh, in_specs=in_specs, out_specs=out_specs, check_vma=False)
```

profile of v0, /device:TPU:1574, one launch (start us, length us, event | category | flops | bytes accessed | tf_op | source)
XLA Modules:
  0.0 289.7 jit_solution(2660515276727011365)
XLA Ops:
  4.2 3.3 %collective-permute-start = (bf16[256,2048]{1,0:T(8,128)(2,1)}, bf16[256,2048]{1,0:T(8,128)(2,1)}, u32[]{:S(2)}, u32[]{:S(2)}) collective-permute-start(bf16[256,2048]{1,0:T(8,128)(2,1)} %param.7), channel_id=1, source_target_pairs={{0,1},{1,2},{2,3},{3,4},{4,5},{5,6},{6,7},{7,8},{8,9},{9,10},{10,1... | collective-permute-start | bytes 3145736 | tf_op jit(solution)/shard_map/ppermute | solution.py:15
  7.5 12.1 %collective-permute-done.6 = bf16[256,2048]{0,1:T(8,128)(2,1)S(1)} collective-permute-done((bf16[256,2048]{0,1:T(8,128)(2,1)S(1)}, bf16[256,2048]{0,1:T(8,128)(2,1)S(1)}, u32[]{:S(2)}, u32[]{:S(2)}) %collective-permute-start.6) | collective-permute-done | bytes 1048608 | tf_op jit(solution)/shard_map/ppermute | solution.py:15
  23.6 3.8 %collective-permute-start.21 = (s32[256]{0:T(256)}, s32[256]{0:T(256)S(1)}, u32[]{:S(2)}, u32[]{:S(2)}) collective-permute-start(s32[256]{0:T(256)} %param.9), channel_id=1, source_target_pairs={{3,0},{4,1},{5,2},{6,3},{7,4},{8,5},{9,6},{10,7},{11,8},{12,9},{13... | collective-permute-start | bytes 3080 | tf_op jit(solution)/shard_map/ppermute | solution.py:15
  27.4 14.7 %collective-permute-done.3 = s32[256]{0:T(256)S(1)} collective-permute-done((s32[256]{0:T(256)}, s32[256]{0:T(256)S(1)}, u32[]{:S(2)}, u32[]{:S(2)}) %collective-permute-start.3) | collective-permute-done | bytes 1056 | tf_op jit(solution)/shard_map/ppermute | solution.py:15
  46.9 4.1 %collective-permute-start.9 = (s32[256]{0:T(256)}, s32[256]{0:T(256)S(1)}, u32[]{:S(2)}, u32[]{:S(2)}) collective-permute-start(s32[256]{0:T(256)} %param.9), channel_id=1, source_target_pairs={{1,0},{2,1},{3,2},{4,3},{5,4},{6,5},{7,6},{8,7},{9,8},{10,9},{11,1... | collective-permute-start | bytes 3080 | tf_op jit(solution)/shard_map/ppermute | solution.py:15
  55.3 4.5 %collective-permute-start.13 = (bf16[256,2048]{1,0:T(8,128)(2,1)}, bf16[256,2048]{1,0:T(8,128)(2,1)}, u32[]{:S(2)}, u32[]{:S(2)}) collective-permute-start(bf16[256,2048]{1,0:T(8,128)(2,1)} %param.8), channel_id=1, source_target_pairs={{1,0},{2,1},{3,2},{4,3},{5,4},{6,5},{7,6},{8,7},{9,8},{10,9},{11,1... | collective-permute-start | bytes 3145736 | tf_op jit(solution)/shard_map/ppermute | solution.py:15
  74.5 6.0 %collective-permute-done.19 = bf16[256,2048]{1,0:T(8,128)(2,1)} collective-permute-done((bf16[256,2048]{1,0:T(8,128)(2,1)}, bf16[256,2048]{1,0:T(8,128)(2,1)}, u32[]{:S(2)}, u32[]{:S(2)}) %collective-permute-start.19) | collective-permute-done | bytes 1048608 | tf_op jit(solution)/shard_map/ppermute | solution.py:15
  85.1 14.6 %collective-permute-done.13 = bf16[256,2048]{1,0:T(8,128)(2,1)} collective-permute-done((bf16[256,2048]{1,0:T(8,128)(2,1)}, bf16[256,2048]{1,0:T(8,128)(2,1)}, u32[]{:S(2)}, u32[]{:S(2)}) %collective-permute-start.13) | collective-permute-done | bytes 1048608 | tf_op jit(solution)/shard_map/ppermute | solution.py:15
  99.7 5.3 %collective-permute-start.10 = (bf16[256,2048]{0,1:T(8,128)(2,1)}, bf16[256,2048]{0,1:T(8,128)(2,1)}, u32[]{:S(2)}, u32[]{:S(2)}) collective-permute-start(bf16[256,2048]{0,1:T(8,128)(2,1)} %copy.74), channel_id=1, source_target_pairs={{1,0},{2,1},{3,2},{4,3},{5,4},{6,5},{7,6},{8,7},{9,8},{10,9},{11,1... | collective-permute-start | bytes 3145736 | tf_op jit(solution)/shard_map/ppermute | solution.py:15
  107.3 25.6 %collective-permute-done.25 = bf16[256,2048]{1,0:T(8,128)(2,1)} collective-permute-done((bf16[256,2048]{1,0:T(8,128)(2,1)}, bf16[256,2048]{1,0:T(8,128)(2,1)}, u32[]{:S(2)}, u32[]{:S(2)}) %collective-permute-start.25) | collective-permute-done | bytes 1048608 | tf_op jit(solution)/shard_map/ppermute | solution.py:15
  132.9 6.2 %collective-permute-start.22 = (bf16[256,2048]{0,1:T(8,128)(2,1)}, bf16[256,2048]{0,1:T(8,128)(2,1)}, u32[]{:S(2)}, u32[]{:S(2)}) collective-permute-start(bf16[256,2048]{0,1:T(8,128)(2,1)} %copy.74), channel_id=1, source_target_pairs={{3,0},{4,1},{5,2},{6,3},{7,4},{8,5},{9,6},{10,7},{11,8},{12,9},{13... | collective-permute-start | bytes 3145736 | tf_op jit(solution)/shard_map/ppermute | solution.py:15
  145.5 9.5 %fusion.3 = (f32[16,256]{1,0:T(8,128)S(1)}, f32[16,1024,256]{2,1,0:T(8,128)}) fusion(pred[256,1024]{0,1:T(8,128)(4,1)S(1)} %compare_and_fusion, bf16[1024,16,128]{0,2,1:T(8,128)(2,1)S(1)} %bitcast.91, bf16[256,16,128]{0,2,1:T(8,128)(2,1)} %bitcast.25), kind=kOutput, calls=%fused_computation.7 | convolution fusion | flops 1086320640 | bytes 22298624 | tf_op jit(solution)/shard_map/ihd,jhd->hij/dot_general | solution.py:46
  155.0 4.0 %collective-permute-start.17 = (f32[16,256]{1,0:T(8,128)S(1)}, f32[16,256]{1,0:T(8,128)S(1)}, u32[]{:S(2)}, u32[]{:S(2)}) collective-permute-start(f32[16,256]{1,0:T(8,128)S(1)} %get-tuple-element.21), channel_id=1, source_target_pairs={{2,0},{3,1},{4,2},{5,3},{6,4},{7,5},{8,6},{9,7},{10,8},{11,9},{12,... | collective-permute-start | bytes 49160 | tf_op jit(solution)/shard_map/ppermute | solution.py:15
  159.0 9.1 %fusion.2 = f32[16,256]{1,0:T(8,128)S(1)} fusion(f32[16,1024,256]{2,1,0:T(8,128)} %get-tuple-element.22, f32[16,256]{1,0:T(8,128)S(1)} %get-tuple-element.21, pred[256,1024]{0,1:T(8,128)(4,1)S(1)} %compare_and_fusion), kind=kLoop, calls=%fused_computation.6 | loop fusion | flops 16773120 | bytes 17072128 | tf_op jit(solution)/shard_map/reduce_sum | solution.py:51
  168.1 10.5 %divide_convert_fusion = bf16[16,256,1024]{1,2,0:T(8,128)(2,1)} fusion(f32[16,1024,256]{2,1,0:T(8,128)} %get-tuple-element.22, f32[16,256]{1,0:T(8,128)S(1)} %fusion.2, f32[16,256]{1,0:T(8,128)S(1)} %get-tuple-element.21, pred[256,1024]{0,1:T(8,128)(4,1)S(1)} %compare_and_fusion), kind=kLoop, calls=%fused_computation.4 | loop fusion | flops 20971520 | bytes 25460736 | tf_op jit(solution)/shard_map/convert_element_type | solution.py:52
  181.5 3.4 %pad_maximum_fusion = bf16[1024,2048]{1,0:T(8,128)(2,1)} fusion(bf16[256,2048]{1,0:T(8,128)(2,1)S(1)} %copy-done.12, bf16[256,2048]{1,0:T(8,128)(2,1)} %collective-permute-done, bf16[256,2048]{1,0:T(8,128)(2,1)} %collective-permute-done.1, bf16[256,2048]{1,0:T(8,128)(2,1)S(1)} %collective-permute-done.2), kind=kLoop, calls=%fused_computation.8 | loop fusion | flops 16777216 | bytes 8388608 | tf_op jit(solution)/shard_map/concatenate | solution.py:35
  184.9 6.4 %copy.33 = bf16[1024,2048]{0,1:T(8,128)(2,1)} copy(bf16[1024,2048]{1,0:T(8,128)(2,1)} %pad_maximum_fusion) | data formatting | bytes 8388608 | tf_op jit(solution)/shard_map/concatenate | solution.py:35
  191.3 6.9 %multiply_reduce_fusion = (f32[256,16]{0,1:T(8,128)S(1)}, bf16[16,128,256]{2,1,0:T(8,128)(2,1)}) fusion(bf16[256,2048]{0,1:T(8,128)(2,1)S(1)} %copy.39, bf16[1024,16,128]{0,2,1:T(8,128)(2,1)} %bitcast.93, bf16[16,256,1024]{1,2,0:T(8,128)(2,1)} %divide_convert_fusion), kind=kOutput, calls=%fused_computation.22 | convolution fusion | flops 1076359168 | bytes 14696448 | tf_op jit(solution)/shard_map/hij,jhd->ihd/dot_general | solution.py:53
  198.2 11.8 %fusion.1 = bf16[16,256,1024]{1,2,0:T(8,128)(2,1)} fusion(bf16[16,256,1024]{1,2,0:T(8,128)(2,1)} %divide_convert_fusion, bf16[1024,16,128]{0,2,1:T(8,128)(2,1)} %bitcast.94, bf16[256,16,128]{0,2,1:T(8,128)(2,1)} %bitcast.98, f32[16,256]{1,0:T(8,128)S(1)} %bitcast.110), kind=kOutput, calls=%fused_computation.2 | convolution fusion | flops 1094713344 | bytes 22036480 | tf_op jit(solution)/shard_map/ihd,jhd->hij/dot_general | solution.py:57
  210.1 5.7 %convolution_convert_fusion = bf16[16,128,256]{2,1,0:T(8,128)(2,1)} fusion(bf16[1024,16,128]{0,2,1:T(8,128)(2,1)S(1)} %bitcast.92, bf16[16,256,1024]{1,2,0:T(8,128)(2,1)} %fusion.1), kind=kOutput, calls=%fused_computation.26 | convolution fusion | flops 1074266112 | bytes 13631488 | tf_op jit(solution)/shard_map/hij,jhd->ihd/dot_general | solution.py:61
  215.8 4.2 %fusion.6 = f32[16,256,128]{1,2,0:T(8,128)} fusion(bf16[256,16,128]{0,2,1:T(8,128)(2,1)} %bitcast.25, bf16[16,256,1024]{1,2,0:T(8,128)(2,1)} %fusion.1), kind=kOutput, calls=%fused_computation.18 | convolution fusion | flops 268435456 | bytes 5242880 | tf_op jit(solution)/shard_map/hij,ihd->jhd/dot_general | solution.py:65
  222.8 4.7 %collective-permute-start.20 = (f32[16,256]{1,0:T(8,128)S(1)}, f32[16,256]{1,0:T(8,128)S(1)}, u32[]{:S(2)}, u32[]{:S(2)}) collective-permute-start(f32[16,256]{1,0:T(8,128)S(1)} %bitcast.111), channel_id=1, source_target_pairs={{2,0},{3,1},{4,2},{5,3},{6,4},{7,5},{8,6},{9,7},{10,8},{11,9},{12,... | collective-permute-start | bytes 49160 | tf_op jit(solution)/shard_map/ppermute | solution.py:15
  237.3 4.6 %collective-permute-start.24 = (f32[16,256]{1,0:T(8,128)S(1)}, f32[16,256]{1,0:T(8,128)S(1)}, u32[]{:S(2)}, u32[]{:S(2)}) collective-permute-start(f32[16,256]{1,0:T(8,128)S(1)} %fusion.2), channel_id=1, source_target_pairs={{3,0},{4,1},{5,2},{6,3},{7,4},{8,5},{9,6},{10,7},{11,8},{12,9},{13... | collective-permute-start | bytes 49160 | tf_op jit(solution)/shard_map/ppermute | solution.py:15
  244.8 4.5 %collective-permute-start.26 = (f32[16,256]{1,0:T(8,128)S(1)}, f32[16,256]{1,0:T(8,128)S(1)}, u32[]{:S(2)}, u32[]{:S(2)}) collective-permute-start(f32[16,256]{1,0:T(8,128)S(1)} %bitcast.113), channel_id=1, source_target_pairs={{3,0},{4,1},{5,2},{6,3},{7,4},{8,5},{9,6},{10,7},{11,8},{12,9},{13... | collective-permute-start | bytes 49160 | tf_op jit(solution)/shard_map/ppermute | solution.py:15
  249.4 3.8 %divide_convert_fusion.3 = bf16[16,256,256]{2,1,0:T(8,128)(2,1)} fusion(f32[16,256]{1,0:T(8,128)S(1)} %get-tuple-element.18, f32[16,256]{1,0:T(8,128)S(1)} %get-tuple-element.17, pred[256,256]{1,0:T(8,128)(4,1)S(1)} %get-tuple-element.14, bf16[256,16,128]{0,2,1:T(8,128)(2,1)} %bitcast.10, bf16[256,2048]{1,0:T(8,128)(2,1)S(1)} %copy-done.13), kind=kOutput, calls=%fused_computation.15 | convolution fusion | flops 273678336 | bytes 4292608 | tf_op jit(solution)/shard_map/ihd,jhd->hij/dot_general | solution.py:85
  253.2 3.9 %divide_convert_fusion.1 = bf16[16,256,256]{2,1,0:T(8,128)(2,1)} fusion(f32[16,256]{1,0:T(8,128)S(1)} %get-tuple-element.16, f32[16,256]{1,0:T(8,128)S(1)} %get-tuple-element.15, pred[256,256]{1,0:T(8,128)(4,1)S(1)} %get-tuple-element.12, bf16[256,16,128]{0,2,1:T(8,128)(2,1)} %bitcast.15, bf16[256,2048]{1,0:T(8,128)(2,1)S(1)} %copy-done.13), kind=kOutput, calls=%fused_computation.11 | convolution fusion | flops 273678336 | bytes 4292608 | tf_op jit(solution)/shard_map/ihd,jhd->hij/dot_general | solution.py:85
  258.9 4.8 %fusion.9 = f32[16,256,128]{1,2,0:T(8,128)} fusion(bf16[256,16,128]{0,2,1:T(8,128)(2,1)} %bitcast.13, bf16[16,256,256]{2,1,0:T(8,128)(2,1)} %copy-done.9, bf16[256,16,128]{0,2,1:T(8,128)(2,1)S(1)} %bitcast.103, bf16[256,16,128]{0,2,1:T(8,128)(2,1)S(1)} %bitcast.95, f32[16,256]{1,0:T(8,128)S(1)} %collective-permute-done.20), kind=kOutput, calls=%fused_computation.24 | convolution fusion | flops 542113792 | bytes 7356416 | tf_op jit(solution)/shard_map/hij,ihd->jhd/dot_general | solution.py:100
  263.7 3.4 %fusion.29 = f32[16,256,128]{1,2,0:T(8,128)} fusion(bf16[256,16,128]{0,2,1:T(8,128)(2,1)S(1)} %bitcast.104, bf16[16,256,256]{2,1,0:T(8,128)(2,1)} %divide_convert_fusion.3), kind=kOutput, calls=%fused_computation.57 | convolution fusion | flops 268435456 | bytes 5242880 | tf_op jit(solution)/shard_map/hij,ihd->jhd/dot_general | solution.py:103
  267.1 4.8 %fusion.8 = f32[16,256,128]{1,2,0:T(8,128)} fusion(bf16[256,16,128]{0,2,1:T(8,128)(2,1)} %bitcast.10, bf16[16,256,256]{2,1,0:T(8,128)(2,1)} %divide_convert_fusion.3, bf16[256,16,128]{0,2,1:T(8,128)(2,1)S(1)} %bitcast.105, bf16[256,16,128]{0,2,1:T(8,128)(2,1)S(1)} %bitcast.96, f32[16,256]{1,0:T(8,128)S(1)} %collective-permute-done.14), kind=kOutput, calls=%fused_computation.23 | convolution fusion | flops 542113792 | bytes 7356416 | tf_op jit(solution)/shard_map/hij,ihd->jhd/dot_general | solution.py:100
  271.9 3.4 %fusion.31 = f32[16,256,128]{1,2,0:T(8,128)} fusion(bf16[256,16,128]{0,2,1:T(8,128)(2,1)S(1)} %bitcast.100, bf16[16,256,256]{2,1,0:T(8,128)(2,1)} %divide_convert_fusion.1), kind=kOutput, calls=%fused_computation.59 | convolution fusion | flops 268435456 | bytes 5242880 | tf_op jit(solution)/shard_map/hij,ihd->jhd/dot_general | solution.py:103
  275.3 6.4 %add_convert_fusion.1 = bf16[16,256,128]{1,2,0:T(8,128)(2,1)} fusion(f32[16,256,128]{1,2,0:T(8,128)} %fusion.9, f32[16,256,128]{1,2,0:T(8,128)} %fusion.6, f32[16,256,128]{1,2,0:T(8,128)} %fusion.8, bf16[256,16,128]{0,2,1:T(8,128)(2,1)} %bitcast.15, bf16[16,256,256]{2,1,0:T(8,128)(2,1)} %divide_convert_fusion.1, bf16[256,16,128]{0,2,1:T(8,128)(2,1)S(1)} %bitcast.101, ...), kind=kOutput, calls=%fused_computation.21 | convolution fusion | flops 544210944 | bytes 12599296 | tf_op jit(solution)/shard_map/hij,ihd->jhd/dot_general | solution.py:100
  284.0 4.3 %add_convert_fusion = bf16[16,256,128]{1,2,0:T(8,128)(2,1)S(1)} fusion(f32[16,256,128]{1,2,0:T(8,128)} %fusion.31, f32[16,256,128]{1,2,0:T(8,128)} %fusion.30, f32[16,256,128]{1,2,0:T(8,128)} %fusion.29, bf16[256,16,128]{0,2,1:T(8,128)(2,1)S(1)} %bitcast.99, bf16[16,256,1024]{1,2,0:T(8,128)(2,1)} %divide_convert_fusion), kind=kOutput, calls=%fused_computation.20 | convolution fusion | flops 270532608 | bytes 10485760 | tf_op jit(solution)/shard_map/hij,ihd->jhd/dot_general | solution.py:68
  (99 shorter events, 68.0 us)
Async XLA Ops:
  0.6 68.5 %copy-start.12 = (bf16[256,2048]{1,0:T(8,128)(2,1)S(1)}, bf16[256,2048]{1,0:T(8,128)(2,1)}, u32[]{:S(2)}) copy-start(bf16[256,2048]{1,0:T(8,128)(2,1)} %param.7) | copy-start | bytes 3145732
  0.6 72.1 %copy-start.16 = (s32[256]{0:T(256)S(1)}, s32[256]{0:T(256)}, u32[]{:S(2)}) copy-start(s32[256]{0:T(256)} %param.9) | copy-start | bytes 3076
  2.2 17.4 %collective-permute-start.6 = (bf16[256,2048]{0,1:T(8,128)(2,1)S(1)}, bf16[256,2048]{0,1:T(8,128)(2,1)S(1)}, u32[]{:S(2)}, u32[]{:S(2)}) collective-permute-start(bf16[256,2048]{0,1:T(8,128)(2,1)S(1)} %copy.34), channel_id=1, source_target_pairs={{0,1},{1,2},{2,3},{3,4},{4,5},{5,6},{6,7},{7,8},{8,9},{9,10},{10,1... | collective-permute-start | bytes 3145736 | tf_op jit(solution)/shard_map/ppermute | solution.py:15
  4.2 58.4 %collective-permute-start = (bf16[256,2048]{1,0:T(8,128)(2,1)}, bf16[256,2048]{1,0:T(8,128)(2,1)}, u32[]{:S(2)}, u32[]{:S(2)}) collective-permute-start(bf16[256,2048]{1,0:T(8,128)(2,1)} %param.7), channel_id=1, source_target_pairs={{0,1},{1,2},{2,3},{3,4},{4,5},{5,6},{6,7},{7,8},{8,9},{9,10},{10,1... | collective-permute-start | bytes 3145736 | tf_op jit(solution)/shard_map/ppermute | solution.py:15
  19.6 48.0 %copy-start.14 = (bf16[256,2048]{0,1:T(8,128)(2,1)}, bf16[256,2048]{0,1:T(8,128)(2,1)S(1)}, u32[]{:S(2)}) copy-start(bf16[256,2048]{0,1:T(8,128)(2,1)S(1)} %collective-permute-done.6) | copy-start | bytes 3145732
  19.6 44.9 %collective-permute-start.7 = (bf16[256,2048]{0,1:T(8,128)(2,1)S(1)}, bf16[256,2048]{0,1:T(8,128)(2,1)}, u32[]{:S(2)}, u32[]{:S(2)}) collective-permute-start(bf16[256,2048]{0,1:T(8,128)(2,1)S(1)} %collective-permute-done.6), channel_id=1, source_target_pairs={{0,1},{1,2},{2,3},{3,4},{4,5},{5,6},{6,7},{7,8},{8,9},{9,10},{10,1... | collective-permute-start | bytes 3145736 | tf_op jit(solution)/shard_map/ppermute | solution.py:15
  21.5 20.6 %collective-permute-start.3 = (s32[256]{0:T(256)}, s32[256]{0:T(256)S(1)}, u32[]{:S(2)}, u32[]{:S(2)}) collective-permute-start(s32[256]{0:T(256)} %param.9), channel_id=1, source_target_pairs={{0,1},{1,2},{2,3},{3,4},{4,5},{5,6},{6,7},{7,8},{8,9},{9,10},{10,1... | collective-permute-start | bytes 3080 | tf_op jit(solution)/shard_map/ppermute | solution.py:15
  23.6 23.3 %collective-permute-start.21 = (s32[256]{0:T(256)}, s32[256]{0:T(256)S(1)}, u32[]{:S(2)}, u32[]{:S(2)}) collective-permute-start(s32[256]{0:T(256)} %param.9), channel_id=1, source_target_pairs={{3,0},{4,1},{5,2},{6,3},{7,4},{8,5},{9,6},{10,7},{11,8},{12,9},{13... | collective-permute-start | bytes 3080 | tf_op jit(solution)/shard_map/ppermute | solution.py:15
  42.2 8.8 %collective-permute-start.4 = (s32[256]{0:T(256)S(1)}, s32[256]{0:T(256)S(1)}, u32[]{:S(2)}, u32[]{:S(2)}) collective-permute-start(s32[256]{0:T(256)S(1)} %collective-permute-done.3), channel_id=1, source_target_pairs={{0,1},{1,2},{2,3},{3,4},{4,5},{5,6},{6,7},{7,8},{8,9},{9,10},{10,1... | collective-permute-start | bytes 3080 | tf_op jit(solution)/shard_map/ppermute | solution.py:15
  44.1 9.0 %collective-permute-start.15 = (s32[256]{0:T(256)}, s32[256]{0:T(256)S(1)}, u32[]{:S(2)}, u32[]{:S(2)}) collective-permute-start(s32[256]{0:T(256)} %param.9), channel_id=1, source_target_pairs={{2,0},{3,1},{4,2},{5,3},{6,4},{7,5},{8,6},{9,7},{10,8},{11,9},{12,... | collective-permute-start | bytes 3080 | tf_op jit(solution)/shard_map/ppermute | solution.py:15
  46.9 8.4 %collective-permute-start.9 = (s32[256]{0:T(256)}, s32[256]{0:T(256)S(1)}, u32[]{:S(2)}, u32[]{:S(2)}) collective-permute-start(s32[256]{0:T(256)} %param.9), channel_id=1, source_target_pairs={{1,0},{2,1},{3,2},{4,3},{5,4},{6,5},{7,6},{8,7},{9,8},{10,9},{11,1... | collective-permute-start | bytes 3080 | tf_op jit(solution)/shard_map/ppermute | solution.py:15
  51.0 8.9 %collective-permute-start.5 = (s32[256]{0:T(256)S(1)}, s32[256]{0:T(256)S(1)}, u32[]{:S(2)}, u32[]{:S(2)}) collective-permute-start(s32[256]{0:T(256)S(1)} %collective-permute-done.4), channel_id=1, source_target_pairs={{0,1},{1,2},{2,3},{3,4},{4,5},{5,6},{6,7},{7,8},{8,9},{9,10},{10,1... | collective-permute-start | bytes 3080 | tf_op jit(solution)/shard_map/ppermute | solution.py:15
  53.1 27.5 %collective-permute-start.19 = (bf16[256,2048]{1,0:T(8,128)(2,1)}, bf16[256,2048]{1,0:T(8,128)(2,1)}, u32[]{:S(2)}, u32[]{:S(2)}) collective-permute-start(bf16[256,2048]{1,0:T(8,128)(2,1)} %param.8), channel_id=1, source_target_pairs={{2,0},{3,1},{4,2},{5,3},{6,4},{7,5},{8,6},{9,7},{10,8},{11,9},{12,... | collective-permute-start | bytes 3145736 | tf_op jit(solution)/shard_map/ppermute | solution.py:15
  55.3 44.3 %collective-permute-start.13 = (bf16[256,2048]{1,0:T(8,128)(2,1)}, bf16[256,2048]{1,0:T(8,128)(2,1)}, u32[]{:S(2)}, u32[]{:S(2)}) collective-permute-start(bf16[256,2048]{1,0:T(8,128)(2,1)} %param.8), channel_id=1, source_target_pairs={{1,0},{2,1},{3,2},{4,3},{5,4},{6,5},{7,6},{8,7},{9,8},{10,9},{11,1... | collective-permute-start | bytes 3145736 | tf_op jit(solution)/shard_map/ppermute | solution.py:15
  59.9 73.0 %collective-permute-start.25 = (bf16[256,2048]{1,0:T(8,128)(2,1)}, bf16[256,2048]{1,0:T(8,128)(2,1)}, u32[]{:S(2)}, u32[]{:S(2)}) collective-permute-start(bf16[256,2048]{1,0:T(8,128)(2,1)} %param.8), channel_id=1, source_target_pairs={{3,0},{4,1},{5,2},{6,3},{7,4},{8,5},{9,6},{10,7},{11,8},{12,9},{13... | collective-permute-start | bytes 3145736 | tf_op jit(solution)/shard_map/ppermute | solution.py:15
  62.6 78.9 %collective-permute-start.1 = (bf16[256,2048]{1,0:T(8,128)(2,1)}, bf16[256,2048]{1,0:T(8,128)(2,1)}, u32[]{:S(2)}, u32[]{:S(2)}) collective-permute-start(bf16[256,2048]{1,0:T(8,128)(2,1)} %collective-permute-done), channel_id=1, source_target_pairs={{0,1},{1,2},{2,3},{3,4},{4,5},{5,6},{6,7},{7,8},{8,9},{9,10},{10,1... | collective-permute-start | bytes 3145736 | tf_op jit(solution)/shard_map/ppermute | solution.py:15
  64.5 78.8 %collective-permute-start.8 = (bf16[256,2048]{0,1:T(8,128)(2,1)}, bf16[256,2048]{0,1:T(8,128)(2,1)}, u32[]{:S(2)}, u32[]{:S(2)}) collective-permute-start(bf16[256,2048]{0,1:T(8,128)(2,1)} %collective-permute-done.7), channel_id=1, source_target_pairs={{0,1},{1,2},{2,3},{3,4},{4,5},{5,6},{6,7},{7,8},{8,9},{9,10},{10,1... | collective-permute-start | bytes 3145736 | tf_op jit(solution)/shard_map/ppermute | solution.py:15
  69.1 122.2 %copy-start.3 = (bf16[256,2048]{0,1:T(8,128)(2,1)}, bf16[256,2048]{0,1:T(8,128)(2,1)S(1)}, u32[]{:S(2)}) copy-start(bf16[256,2048]{0,1:T(8,128)(2,1)S(1)} %copy.39) | copy-start | bytes 3145732
  80.6 149.8 %collective-permute-start.16 = (bf16[256,2048]{0,1:T(8,128)(2,1)}, bf16[256,2048]{0,1:T(8,128)(2,1)}, u32[]{:S(2)}, u32[]{:S(2)}) collective-permute-start(bf16[256,2048]{0,1:T(8,128)(2,1)} %copy.74), channel_id=1, source_target_pairs={{2,0},{3,1},{4,2},{5,3},{6,4},{7,5},{8,6},{9,7},{10,8},{11,9},{12,... | collective-permute-start | bytes 3145736 | tf_op jit(solution)/shard_map/ppermute | solution.py:15
  99.7 149.7 %collective-permute-start.10 = (bf16[256,2048]{0,1:T(8,128)(2,1)}, bf16[256,2048]{0,1:T(8,128)(2,1)}, u32[]{:S(2)}, u32[]{:S(2)}) collective-permute-start(bf16[256,2048]{0,1:T(8,128)(2,1)} %copy.74), channel_id=1, source_target_pairs={{1,0},{2,1},{3,2},{4,3},{5,4},{6,5},{7,6},{8,7},{9,8},{10,9},{11,1... | collective-permute-start | bytes 3145736 | tf_op jit(solution)/shard_map/ppermute | solution.py:15
  132.9 120.3 %collective-permute-start.22 = (bf16[256,2048]{0,1:T(8,128)(2,1)}, bf16[256,2048]{0,1:T(8,128)(2,1)}, u32[]{:S(2)}, u32[]{:S(2)}) collective-permute-start(bf16[256,2048]{0,1:T(8,128)(2,1)} %copy.74), channel_id=1, source_target_pairs={{3,0},{4,1},{5,2},{6,3},{7,4},{8,5},{9,6},{10,7},{11,8},{12,9},{13... | collective-permute-start | bytes 3145736 | tf_op jit(solution)/shard_map/ppermute | solution.py:15
  141.4 37.3 %collective-permute-start.2 = (bf16[256,2048]{1,0:T(8,128)(2,1)}, bf16[256,2048]{1,0:T(8,128)(2,1)S(1)}, u32[]{:S(2)}, u32[]{:S(2)}) collective-permute-start(bf16[256,2048]{1,0:T(8,128)(2,1)} %collective-permute-done.1), channel_id=1, source_target_pairs={{0,1},{1,2},{2,3},{3,4},{4,5},{5,6},{6,7},{7,8},{8,9},{9,10},{10,1... | collective-permute-start | bytes 3145736 | tf_op jit(solution)/shard_map/ppermute | solution.py:15
  155.0 67.8 %collective-permute-start.17 = (f32[16,256]{1,0:T(8,128)S(1)}, f32[16,256]{1,0:T(8,128)S(1)}, u32[]{:S(2)}, u32[]{:S(2)}) collective-permute-start(f32[16,256]{1,0:T(8,128)S(1)} %get-tuple-element.21), channel_id=1, source_target_pairs={{2,0},{3,1},{4,2},{5,3},{6,4},{7,5},{8,6},{9,7},{10,8},{11,9},{12,... | collective-permute-start | bytes 49160 | tf_op jit(solution)/shard_map/ppermute | solution.py:15
  178.7 48.9 %collective-permute-start.18 = (f32[16,256]{1,0:T(8,128)S(1)}, f32[16,256]{1,0:T(8,128)S(1)}, u32[]{:S(2)}, u32[]{:S(2)}) collective-permute-start(f32[16,256]{1,0:T(8,128)S(1)} %fusion.2), channel_id=1, source_target_pairs={{2,0},{3,1},{4,2},{5,3},{6,4},{7,5},{8,6},{9,7},{10,8},{11,9},{12,... | collective-permute-start | bytes 49160 | tf_op jit(solution)/shard_map/ppermute | solution.py:15
  222.8 36.1 %collective-permute-start.20 = (f32[16,256]{1,0:T(8,128)S(1)}, f32[16,256]{1,0:T(8,128)S(1)}, u32[]{:S(2)}, u32[]{:S(2)}) collective-permute-start(f32[16,256]{1,0:T(8,128)S(1)} %bitcast.111), channel_id=1, source_target_pairs={{2,0},{3,1},{4,2},{5,3},{6,4},{7,5},{8,6},{9,7},{10,8},{11,9},{12,... | collective-permute-start | bytes 49160 | tf_op jit(solution)/shard_map/ppermute | solution.py:15
  227.6 7.7 %collective-permute-start.11 = (f32[16,256]{1,0:T(8,128)S(1)}, f32[16,256]{1,0:T(8,128)S(1)}, u32[]{:S(2)}, u32[]{:S(2)}) collective-permute-start(f32[16,256]{1,0:T(8,128)S(1)} %get-tuple-element.21), channel_id=1, source_target_pairs={{1,0},{2,1},{3,2},{4,3},{5,4},{6,5},{7,6},{8,7},{9,8},{10,9},{11,1... | collective-permute-start | bytes 49160 | tf_op jit(solution)/shard_map/ppermute | solution.py:15
  230.4 6.9 %collective-permute-start.12 = (f32[16,256]{1,0:T(8,128)S(1)}, f32[16,256]{1,0:T(8,128)S(1)}, u32[]{:S(2)}, u32[]{:S(2)}) collective-permute-start(f32[16,256]{1,0:T(8,128)S(1)} %fusion.2), channel_id=1, source_target_pairs={{1,0},{2,1},{3,2},{4,3},{5,4},{6,5},{7,6},{8,7},{9,8},{10,9},{11,1... | collective-permute-start | bytes 49160 | tf_op jit(solution)/shard_map/ppermute | solution.py:15
  235.2 21.9 %copy-start.9 = (bf16[16,256,256]{2,1,0:T(8,128)(2,1)}, bf16[16,256,256]{2,1,0:T(8,128)(2,1)S(1)}, u32[]{:S(2)}) copy-start(bf16[16,256,256]{2,1,0:T(8,128)(2,1)S(1)} %divide_convert_fusion.2) | copy-start | bytes 6291460
  235.2 6.7 %collective-permute-start.23 = (f32[16,256]{1,0:T(8,128)S(1)}, f32[16,256]{1,0:T(8,128)S(1)}, u32[]{:S(2)}, u32[]{:S(2)}) collective-permute-start(f32[16,256]{1,0:T(8,128)S(1)} %get-tuple-element.21), channel_id=1, source_target_pairs={{3,0},{4,1},{5,2},{6,3},{7,4},{8,5},{9,6},{10,7},{11,8},{12,9},{13... | collective-permute-start | bytes 49160 | tf_op jit(solution)/shard_map/ppermute | solution.py:15
  237.3 7.5 %collective-permute-start.24 = (f32[16,256]{1,0:T(8,128)S(1)}, f32[16,256]{1,0:T(8,128)S(1)}, u32[]{:S(2)}, u32[]{:S(2)}) collective-permute-start(f32[16,256]{1,0:T(8,128)S(1)} %fusion.2), channel_id=1, source_target_pairs={{3,0},{4,1},{5,2},{6,3},{7,4},{8,5},{9,6},{10,7},{11,8},{12,9},{13... | collective-permute-start | bytes 49160 | tf_op jit(solution)/shard_map/ppermute | solution.py:15
  242.0 25.2 %collective-permute-start.14 = (f32[16,256]{1,0:T(8,128)S(1)}, f32[16,256]{1,0:T(8,128)S(1)}, u32[]{:S(2)}, u32[]{:S(2)}) collective-permute-start(f32[16,256]{1,0:T(8,128)S(1)} %bitcast.112), channel_id=1, source_target_pairs={{1,0},{2,1},{3,2},{4,3},{5,4},{6,5},{7,6},{8,7},{9,8},{10,9},{11,1... | collective-permute-start | bytes 49160 | tf_op jit(solution)/shard_map/ppermute | solution.py:15
  244.8 30.5 %collective-permute-start.26 = (f32[16,256]{1,0:T(8,128)S(1)}, f32[16,256]{1,0:T(8,128)S(1)}, u32[]{:S(2)}, u32[]{:S(2)}) collective-permute-start(f32[16,256]{1,0:T(8,128)S(1)} %bitcast.113), channel_id=1, source_target_pairs={{3,0},{4,1},{5,2},{6,3},{7,4},{8,5},{9,6},{10,7},{11,8},{12,9},{13... | collective-permute-start | bytes 49160 | tf_op jit(solution)/shard_map/ppermute | solution.py:15
  (12 other events, 91.9 us)
where the time goes:
time: 291 us; the launch traced here: 290 us
  starting transfers between devices  84.4 us (29%)
  matrix products  77.5 us (27%)
  waiting for transfers between devices  73.1 us (25%)
  other arithmetic  27.1 us (9%)
  local copies, waits for them, and re-layouts  26.5 us (9%)
    ppermute x27, starting transfers between devices, shifted(): return lax.ppermute(x, axis, pairs)  84.4 us
    ppermute x27, waiting for transfers between devices, shifted(): return lax.ppermute(x, axis, pairs)  73.1 us
    dot_general x3, matrix products, local(): jnp.einsum('hij,ihd->jhd', far_dscore, far_query3, preferred_element_type...  16 us
    dot_general x1, matrix products, local(): jnp.einsum('ihd,jhd->hij', grad3, value_all, preferred_element_type=jnp.f...  11.8 us
    convert_element_type x1, other arithmetic, local(): weights = (exponent / row_total).astype(jnp.bfloat16)  10.5 us
    dot_general x3, matrix products, local(): jnp.einsum('ihd,jhd->hij', far_query3, own_keys, preferred_element_type=j...  10.5 us
    unnamed x40, local copies, waits for them, and re-layouts  9.63 us
    dot_general x1, matrix products, local(): jnp.einsum('ihd,jhd->hij', query3, key_all, preferred_element_type=jnp.fl...  9.49 us
  transfers between devices with their start and end apart: 27, of which 5 were waited for; matrix products, arithmetic and copies ran while one was open for 40% of the time, Pallas kernels for 0%

commit v1 on v0

v1 whole, which is shorter than its diff:
```python
import functools
import math

import jax
import jax.numpy as jnp
from jax import lax
from jax.experimental import pallas as pl
from jax.experimental.pallas import tpu as pltpu
from jax.sharding import PartitionSpec as P

HEADS = 16
MESH = pl.DeviceIdType.MESH
DELAY = 3
NEG = -1e30
F32 = jnp.float32
BF16 = jnp.bfloat16


def dot_nt(a, b):
    return lax.dot_general(a, b, (((1,), (1,)), ((), ())), preferred_element_type=F32)


def dot_nn(a, b):
    return lax.dot_general(a, b, (((1,), (0,)), ((), ())), preferred_element_type=F32)


def dot_tn(a, b):
    return lax.dot_general(a, b, (((0,), (0,)), ((), ())), preferred_element_type=F32)


def colsum(x):
    return jnp.sum(x, axis=0, keepdims=True)


def colmax(x):
    return jnp.max(x, axis=0, keepdims=True)


def kernel(
    n,
    q_h, k_h, v_h, g_h, seg_h,
    o_h, dq_h, dk_h, dv_h,
    q_all, k_all, v_all, g_all, seg_buf, flags,
    b_own, b_left, b_right, b_far,
    rp, rm, sendp, sendm,
    st_own, st_in, st_tot, st_ret, st_fin,
    acc_o, acc_dq, acc_dk, acc_dv, staged,
    in_loc, in_snd, in_rcv, seg_sem,
    p_snd, p_rcv, m_snd, m_rcv,
    a_snd, a_rcv, f_snd, f_rcv,
    out_loc, out_snd, out_rcv,
):
    tok, feature = q_h.shape
    heads = HEADS // 2
    hd = feature // HEADS
    own = 2 * tok
    span = own - hd
    scale = math.log2(math.e) / math.sqrt(hd)
    inv_root = 1.0 / math.sqrt(hd)
    wide = 2 * hd

    me = lax.axis_index("seq")
    core = lax.rem(me, 2)
    partner = me + 1 - 2 * core
    left = lax.rem(me + n - 2, n)
    right = lax.rem(me + 2, n)

    barrier = pltpu.get_barrier_semaphore()
    for peer in (partner, left, right):
        pl.semaphore_signal(barrier, inc=1, device_id={"seq": peer}, device_id_type=MESH)
    pl.semaphore_wait(barrier, 3)

    def remote(src, dst, snd, rcv, peer):
        return pltpu.make_async_remote_copy(
            src_ref=src, dst_ref=dst, send_sem=snd, recv_sem=rcv,
            device_id={"seq": peer}, device_id_type=MESH,
        )

    mine = pl.ds(pl.multiple_of(core * tok, tok), tok)
    theirs = pl.ds(pl.multiple_of((1 - core) * tok, tok), tok)
    pairs_in = ((k_h, k_all), (v_h, v_all), (q_h, q_all), (g_h, g_all))

    def columns(which, h):
        return pl.ds(pl.multiple_of((which * heads + h) * hd, hd), hd)

    def in_local(j, h):
        src, dst = pairs_in[j]
        return pltpu.make_async_copy(src.at[:, columns(core, h)], dst.at[h, mine], in_loc.at[j, h])

    def in_remote(j, h):
        src, dst = pairs_in[j]
        return remote(
            src.at[:, columns(1 - core, h)], dst.at[h, mine], in_snd.at[j, h], in_rcv.at[j, h], partner
        )

    seg_local = pltpu.make_async_copy(seg_h, seg_buf.at[0, core], seg_sem.at[0])
    seg_remote = remote(seg_h, seg_buf.at[0, core], seg_sem.at[1], seg_sem.at[2], partner)
    seg_right = remote(seg_buf.at[0], seg_buf.at[1], seg_sem.at[3], seg_sem.at[4], right)
    seg_left = remote(seg_buf.at[0], seg_buf.at[2], seg_sem.at[5], seg_sem.at[6], left)
    seg_local.start()
    seg_remote.start()

    def start_inputs(h, _):
        for j in range(4):
            in_remote(j, h).start()
            in_local(j, h).start()
        return 0

    lax.fori_loop(0, heads, start_inputs, 0)

    def wait_inputs(h):
        for j in range(4):
            in_local(j, h).wait()
            in_remote(j, h).wait_recv()

    def early(t):
        tail, head = pl.ds(own - span, span), pl.ds(0, span)
        return (
            remote(k_all.at[t, tail], rp.at[t, 0], p_snd.at[t, 0], p_rcv.at[t, 0], right),
            remote(q_all.at[t, head], rm.at[t, 0], m_snd.at[t, 0], m_rcv.at[t, 0], left),
            remote(v_all.at[t, tail], rp.at[t, 1], p_snd.at[t, 1], p_rcv.at[t, 1], right),
            remote(g_all.at[t, head], rm.at[t, 1], m_snd.at[t, 1], m_rcv.at[t, 1], left),
        )

    def late(h):
        t = h + DELAY
        return (
            remote(sendp.at[h, 0], rp.at[t, 0], p_snd.at[t, 0], p_rcv.at[t, 0], right),
            remote(sendp.at[h, 1], rp.at[t, 1], p_snd.at[t, 1], p_rcv.at[t, 1], right),
            remote(st_ret.at[h], st_fin.at[h], f_snd.at[h], f_rcv.at[h], right),
            remote(sendm.at[h, 0], rm.at[t, 0], m_snd.at[t, 0], m_rcv.at[t, 0], left),
            remote(sendm.at[h, 1], rm.at[t, 1], m_snd.at[t, 1], m_rcv.at[t, 1], left),
        )

    def stats(h):
        return remote(st_own.at[h], st_in.at[h], a_snd.at[h], a_rcv.at[h], left)

    def start_early(t, _):
        wait_inputs(t)
        for copy in early(t):
            copy.start()
        return 0

    start_early(0, 0)
    seg_local.wait()
    seg_remote.wait_recv()
    seg_right.start()
    seg_left.start()
    lax.fori_loop(1, DELAY, start_early, 0)

    def rows(ref, h, first, blocks):
        parts = [ref[h, first + b : first + b + 1, :] for b in range(blocks)]
        return parts[0] if blocks == 1 else jnp.concatenate(parts, axis=1)

    def put_rows(ref, h, first, value):
        for b in range(value.shape[1] // hd):
            ref[h, first + b : first + b + 1, :] = value[:, b * hd : (b + 1) * hd]

    def own_stats(h):
        for b in range(2):
            depth = (b + 1) * wide
            at = slice(b * wide, (b + 1) * wide)
            s = dot_nt(k_all[h, :depth], q_all[h, at]) * scale + b_own[:depth, at]
            dp = dot_nt(v_all[h, :depth], g_all[h, at])
            m = colmax(s)
            p = jnp.exp2(s - m)
            total = colsum(p)
            put_rows(st_own, h, 2 * b, m + jnp.log2(total))
            put_rows(st_own, h, 4 + 2 * b, colsum(p * dp) / total)

    def finish(s, dp, lse, delta):
        p = jnp.exp2(s - lse)
        return p.astype(BF16), (p * ((dp - delta) * inv_root)).astype(BF16)

    def merge(lse, delta, parts):
        m = lse
        for s, _ in parts:
            m = jnp.maximum(m, colmax(s))
        first = jnp.exp2(lse - m)
        total, dn = first, delta * first
        probs = []
        for s, dp in parts:
            p = jnp.exp2(s - m)
            total = total + colsum(p)
            dn = dn + colsum(p * dp)
            probs.append(p)
        inv = 1.0 / total
        delta = dn * inv
        outs = []
        for p, (_, dp) in zip(probs, parts):
            p = p * inv
            outs.append((p.astype(BF16), (p * ((dp - delta) * inv_root)).astype(BF16)))
        return m + jnp.log2(total), delta, outs

    def cross(h):
        cut = span - wide
        nxt = jnp.minimum(h + DELAY, heads - 1)
        fresh = jnp.where(h + DELAY < heads, 1.0, 0.0)
        keys_right = jnp.broadcast_to((1.0 - flags[1:2, :]) * fresh, (span, hd)) > 0.5
        queries_left = jnp.broadcast_to(flags[0:1, :] * fresh, (span, hd)) > 0.5
        kl, vl = rp[h, 0], rp[h, 1]
        k, v = k_all[h], v_all[h]
        qa, ga = rm[h, 0, :wide], rm[h, 1, :wide]
        s1 = dot_nt(k, qa) * scale + b_right[:, :wide]
        s2 = dot_nt(kl[cut:], qa) * scale + b_far[...]
        d1, d2 = dot_nt(v, ga), dot_nt(vl[cut:], ga)
        lse, delta, ((p1, e1), (p2, e2)) = merge(
            rows(st_in, h, 0, 2), rows(st_in, h, 4, 2), ((s1, d1), (s2, d2))
        )
        put_rows(st_ret, h, 0, lse)
        put_rows(st_ret, h, 4, delta)
        dk, dv = dot_nn(e1, qa), dot_nn(p1, ga)
        dkl, dvl = dot_nn(e2, qa), dot_nn(p2, ga)
        for i, (a1, b1, a2, b2, kept) in enumerate(
            ((p1, v, p2, vl[cut:], k_all), (e1, k, e2, kl[cut:], v_all))
        ):
            part = dot_tn(a1, b1) + dot_tn(a2, b2)
            stay = kept[nxt, own - span : own - span + wide].astype(F32)
            sendp[h, i, :wide] = jnp.where(keys_right[:wide], stay, part).astype(BF16)
        qb, gb = rm[h, 0, wide:], rm[h, 1, wide:]
        s3 = dot_nt(k, qb) * scale + b_right[:, wide:]
        d3 = dot_nt(v, gb)
        lse, delta, ((p3, e3),) = merge(rows(st_in, h, 2, 1), rows(st_in, h, 6, 1), ((s3, d3),))
        put_rows(st_ret, h, 2, lse)
        put_rows(st_ret, h, 6, delta)
        acc_dk[h] = dk + dot_nn(e3, qb)
        acc_dv[h] = dv + dot_nn(p3, gb)
        for i, (a3, b3, kept) in enumerate(((p3, v, k_all), (e3, k, v_all))):
            part = dot_tn(a3, b3)
            stay = kept[nxt, own - span + wide :].astype(F32)
            sendp[h, i, wide:] = jnp.where(keys_right[wide:], stay, part).astype(BF16)
        dkl_sum = dvl_sum = None
        for b in range(2):
            at = slice(b * wide, (b + 1) * wide)
            q, g = q_all[h, at], g_all[h, at]
            s = dot_nt(kl, q) * scale + b_left[:, at]
            dp = dot_nt(vl, g)
            lse, delta, ((p, e),) = merge(
                rows(st_own, h, 2 * b, 2), rows(st_own, h, 4 + 2 * b, 2), ((s, dp),)
            )
            put_rows(st_tot, h, 2 * b, lse)
            put_rows(st_tot, h, 4 + 2 * b, delta)
            acc_o[h, at] = dot_tn(p, vl)
            acc_dq[h, at] = dot_tn(e, kl)
            dkb, dvb = dot_nn(e, q), dot_nn(p, g)
            dkl_sum = dkb if b == 0 else dkl_sum + dkb
            dvl_sum = dvb if b == 0 else dvl_sum + dvb
        for i, (total, extra, kept) in enumerate(((dkl_sum, dkl, q_all), (dvl_sum, dvl, g_all))):
            stay = kept[nxt, :span].astype(F32)
            sendm[h, i, :cut] = jnp.where(queries_left[:cut], stay[:cut], total[:cut]).astype(BF16)
            sendm[h, i, cut:] = jnp.where(
                queries_left[cut:], stay[cut:], total[cut:] + extra
            ).astype(BF16)

    def close(h):
        t = h + DELAY
        asked = flags[0:1, :] > 0.5
        back = jnp.broadcast_to(flags[0:1, :], (span, hd)) > 0.5
        back_keys = jnp.broadcast_to(1.0 - flags[1:2, :], (span, hd)) > 0.5
        lse = [st_tot[h, b : b + 1, :] for b in range(4)]
        delta = [st_tot[h, 4 + b : 5 + b, :] for b in range(4)]
        for b in range(3):
            lse[b] = jnp.where(asked, st_fin[h, b : b + 1, :], lse[b])
            delta[b] = jnp.where(asked, st_fin[h, 4 + b : 5 + b, :], delta[b])
        add = [jnp.where(back, rp[t, i].astype(F32), 0.0) for i in range(2)]
        for b in range(2):
            depth = (b + 1) * wide
            at = slice(b * wide, (b + 1) * wide)
            q, g, k, v = q_all[h, at], g_all[h, at], k_all[h, :depth], v_all[h, :depth]
            s = dot_nt(k, q) * scale + b_own[:depth, at]
            dp = dot_nt(v, g)
            p, e = finish(
                s, dp, jnp.concatenate(lse[2 * b : 2 * b + 2], 1), jnp.concatenate(delta[2 * b : 2 * b + 2], 1)
            )
            acc_dk[h, :depth] += dot_nn(e, q)
            acc_dv[h, :depth] += dot_nn(p, g)
            for i, (value, acc) in enumerate(((dot_tn(p, v), acc_o), (dot_tn(e, k), acc_dq))):
                value = value + acc[h, at]
                if b == 0:
                    staged[h, i, at] = (value + add[i][:wide]).astype(BF16)
                else:
                    staged[h, i, wide:span] = (value[: span - wide] + add[i][wide:]).astype(BF16)
                    staged[h, i, span:] = value[span - wide :].astype(BF16)
        for i, acc in ((0, acc_dk), (1, acc_dv)):
            staged[h, 2 + i, : own - span] = acc[h, : own - span].astype(BF16)
            staged[h, 2 + i, own - span :] = (
                acc[h, own - span :] + jnp.where(back_keys, rm[t, i].astype(F32), 0.0)
            ).astype(BF16)

    outs = (o_h, dq_h, dk_h, dv_h)

    def out_local(j, h):
        return pltpu.make_async_copy(
            staged.at[h, j, mine], outs[j].at[:, columns(core, h)], out_loc.at[j, h]
        )

    def out_remote(j, h):
        return remote(
            staged.at[h, j, theirs], outs[j].at[:, columns(core, h)],
            out_snd.at[j, h], out_rcv.at[j, h], partner,
        )

    seg_right.wait_recv()
    seg_left.wait_recv()

    def seg_row(chip, b):
        return seg_buf[chip, b // 2, b % 2 : b % 2 + 1, :].astype(F32)

    def seg_at(chip, b, lane):
        return jnp.broadcast_to(seg_row(chip, b)[:, lane : lane + 1], (1, hd))

    asks_left = seg_at(1, 0, hd - 1) == seg_at(0, 0, 0)
    asks_right = seg_at(0, 0, hd - 1) == seg_at(2, 0, 0)
    flags[0:1, :] = jnp.where(asks_left, 1.0, 0.0)
    flags[1:2, :] = jnp.where(asks_right, 1.0, 0.0)

    def as_column(row):
        return jnp.transpose(jnp.broadcast_to(row, (hd, hd)))

    own_rows = [seg_row(0, b) for b in range(4)]
    own_cols = [as_column(row) for row in own_rows]
    left_cols = [as_column(jnp.where(asks_left, -1.0, seg_row(1, b + 1))) for b in range(3)]
    right_rows = [jnp.where(asks_right, seg_row(2, b), -2.0) for b in range(3)]
    causal = lax.broadcasted_iota(jnp.int32, (hd, hd), 0) <= lax.broadcasted_iota(jnp.int32, (hd, hd), 1)

    def tile(a, b):
        return slice(a * hd, (a + 1) * hd), slice(b * hd, (b + 1) * hd)

    for a in range(4):
        for b in range(4):
            if a > b:
                b_own[tile(a, b)] = jnp.full((hd, hd), NEG, F32)
            else:
                same = own_cols[a] == own_rows[b]
                b_own[tile(a, b)] = jnp.where(same & causal if a == b else same, 0.0, NEG)
            if a < 3:
                b_left[tile(a, b)] = jnp.where(left_cols[a] == own_rows[b], 0.0, NEG)
            if b < 3:
                b_right[tile(a, b)] = jnp.where(own_cols[a] == right_rows[b], 0.0, NEG)
            if a < 2 and b < 2:
                b_far[tile(a, b)] = jnp.where(left_cols[a + 1] == right_rows[b], 0.0, NEG)

    own_stats(0)
    stats(0).start()

    def step(i, _):
        @pl.when(i + 1 < heads)
        def _():
            own_stats(i + 1)
            stats(i + 1).start()

        @pl.when(i + DELAY < heads)
        def _():
            wait_inputs(i + DELAY)

        for j in range(2):
            remote(sendp.at[0, j], rp.at[i, j], p_snd.at[i, j], p_rcv.at[i, j], right).wait_recv()
            remote(sendm.at[0, j], rm.at[i, j], m_snd.at[i, j], m_rcv.at[i, j], left).wait_recv()

        @pl.when(i < heads)
        def _():
            stats(i).wait_recv()
            cross(i)
            for copy in late(i):
                copy.start()

        @pl.when(i >= DELAY)
        def _():
            h = i - DELAY
            remote(st_ret.at[h], st_fin.at[h], f_snd.at[h], f_rcv.at[h], right).wait_recv()
            close(h)
            for j in range(4):
                out_remote(j, h).start()
                out_local(j, h).start()

        return 0

    lax.fori_loop(0, heads + DELAY, step, 0)

    def drain(h, _):
        for j in range(4):
            in_remote(j, h).wait_send()
            out_local(j, h).wait()
            out_remote(j, h).wait()
        stats(h).wait_send()
        for copy in late(h):
            copy.wait_send()
        return 0

    def drain_early(t, _):
        for copy in early(t):
            copy.wait_send()
        return 0

    lax.fori_loop(0, heads, drain, 0)
    lax.fori_loop(0, DELAY, drain_early, 0)
    seg_remote.wait_send()
    seg_right.wait_send()
    seg_left.wait_send()


def local(n, queries, keys, values, out_grad, segments):
    tok, feature = queries.shape
    heads, hd = HEADS // 2, feature // HEADS
    own = 2 * tok
    span = own - hd
    slots = heads + DELAY
    out = jax.ShapeDtypeStruct((tok, feature), BF16)
    dma = pltpu.SemaphoreType.DMA
    vm = pltpu.VMEM
    return pl.pallas_call(
        functools.partial(kernel, n),
        out_shape=(out,) * 4,
        in_specs=[pl.BlockSpec(memory_space=pl.ANY)] * 5,
        out_specs=[pl.BlockSpec(memory_space=pl.ANY)] * 4,
        scratch_shapes=[
            vm((heads, own, hd), BF16), vm((heads, own, hd), BF16),
            vm((heads, own, hd), BF16), vm((heads, own, hd), BF16),
            vm((3, 2, 2, hd), jnp.int32), vm((8, hd), F32),
            vm((own, own), F32), vm((span, own), F32), vm((own, span), F32), vm((2 * hd, 2 * hd), F32),
            vm((slots, 2, span, hd), BF16), vm((slots, 2, span, hd), BF16),
            vm((heads, 2, span, hd), BF16), vm((heads, 2, span, hd), BF16),
            vm((heads, 8, hd), F32), vm((heads, 8, hd), F32), vm((heads, 8, hd), F32),
            vm((heads, 8, hd), F32), vm((heads, 8, hd), F32),
            vm((heads, own, hd), F32), vm((heads, own, hd), F32),
            vm((heads, own, hd), F32), vm((heads, own, hd), F32),
            vm((heads, 4, own, hd), BF16),
            dma((4, heads)), dma((4, heads)), dma((4, heads)), dma((7,)),
            dma((slots, 2)), dma((slots, 2)), dma((slots, 2)), dma((slots, 2)),
            dma((heads,)), dma((heads,)), dma((heads,)), dma((heads,)),
            dma((4, heads)), dma((4, heads)), dma((4, heads)),
        ],
        compiler_params=pltpu.CompilerParams(
            collective_id=0, has_side_effects=True, vmem_limit_bytes=60 * 2**20
        ),
        name="packed_attention",
    )(queries, keys, values, out_grad, segments.reshape(2, tok // 2))


def solution(mesh):
    spec = P(("branch", "seq"), None)
    return jax.shard_map(
        functools.partial(local, mesh.shape["seq"]),
        mesh=mesh,
        in_specs=(spec,) * 4 + (P(("branch", "seq")),),
        out_specs=(spec,) * 4,
        check_vma=False,
    )
```

time: 291 us -> 93.9 us (0.32)
  the two profiles are of different devices: /device:TPU:1574 before, /device:TPU:37 now
where the time goes in v1:
time: 93.9 us; the launch traced here: 93.6 us
  Pallas kernels  86.4 us (92%)
  local copies, waits for them, and re-layouts  6.57 us (7%)
    pallas_call x1, Pallas kernels, local(): pl.pallas_call(functools.partial(kernel, n), out_shape=(out,) * 4, in_spe...  86.4 us
    unnamed x10, local copies, waits for them, and re-layouts  6.57 us

profile of v1, /device:TPU:37, one launch (start us, length us, event | category | flops | bytes accessed | tf_op | source)
XLA Modules:
  0.0 93.6 jit_solution(10933901909072117427)
XLA Ops:
  0.6 86.4 %packed_attention.1 = (bf16[256,2048]{1,0:T(8,128)(2,1)}, bf16[256,2048]{1,0:T(8,128)(2,1)}, bf16[256,2048]{1,0:T(8,128)(2,1)}, bf16[256,2048]{1,0:T(8,128)(2,1)}) custom-call(bf16[256,2048]{1,0:T(8,128)(2,1)} %q_h.1, bf16[256,2048]{1,0:T(8,128)(2,1)} %k_h.1, bf16[256,2048]{1,0:T(8,128)(2,1)} %v_h.1, bf16[256,2048]{1,0:T(8,128)(2,1)} %g_h.1, s32[2,128]{1,0:T(2,128)} %bitcast.1), custom_call_target="tpu_custom_call" | custom-call | tf_op jit(solution)/shard_map/packed_attention/pallas_call | solution.py:411
  87.0 0.0 copy-start.2
  87.0 2.4 %copy.13 = bf16[256,2048]{1,0:T(8,128)(2,1)} copy(bf16[256,2048]{1,0:T(8,128)(2,1)} %get-tuple-element.8) | data formatting | bytes 2097152
  89.4 0.0 copy-done.2
  89.4 0.0 copy-start.1
  89.4 1.0 %copy.14 = bf16[256,2048]{1,0:T(8,128)(2,1)} copy(bf16[256,2048]{1,0:T(8,128)(2,1)S(1)} %copy-done.2) | data formatting | bytes 2097152
  90.4 0.6 copy-done.1
  91.0 0.0 copy-start
  91.0 1.0 %copy.15 = bf16[256,2048]{1,0:T(8,128)(2,1)} copy(bf16[256,2048]{1,0:T(8,128)(2,1)S(1)} %copy-done.1) | data formatting | bytes 2097152
  92.0 0.6 copy-done
  92.6 1.0 %copy.16 = bf16[256,2048]{1,0:T(8,128)(2,1)} copy(bf16[256,2048]{1,0:T(8,128)(2,1)S(1)} %copy-done) | data formatting | bytes 2097152
Async XLA Ops:
  87.0 2.4 %copy-start.2 = (bf16[256,2048]{1,0:T(8,128)(2,1)S(1)}, bf16[256,2048]{1,0:T(8,128)(2,1)}, u32[]{:S(2)}) copy-start(bf16[256,2048]{1,0:T(8,128)(2,1)} %get-tuple-element.9) | copy-start | bytes 3145732
  89.4 1.6 %copy-start.1 = (bf16[256,2048]{1,0:T(8,128)(2,1)S(1)}, bf16[256,2048]{1,0:T(8,128)(2,1)}, u32[]{:S(2)}) copy-start(bf16[256,2048]{1,0:T(8,128)(2,1)} %get-tuple-element.10) | copy-start | bytes 3145732
  91.0 1.6 %copy-start = (bf16[256,2048]{1,0:T(8,128)(2,1)S(1)}, bf16[256,2048]{1,0:T(8,128)(2,1)}, u32[]{:S(2)}) copy-start(bf16[256,2048]{1,0:T(8,128)(2,1)} %get-tuple-element.11) | copy-start | bytes 3145732

commit v2 on v1

v2 whole, which is shorter than its diff:
```python
import functools
import math

import jax
import jax.numpy as jnp
from jax import lax
from jax.experimental import pallas as pl
from jax.experimental.pallas import tpu as pltpu
from jax.sharding import PartitionSpec as P

HEADS = 16
MESH = pl.DeviceIdType.MESH
DELAY = 2
NEG = -1e30
STAT = 16
F32 = jnp.float32
BF16 = jnp.bfloat16


def dot_nt(a, b):
    return lax.dot_general(a, b, (((1,), (1,)), ((), ())), preferred_element_type=F32)


def dot_nn(a, b):
    return lax.dot_general(a, b, (((1,), (0,)), ((), ())), preferred_element_type=F32)


def dot_tn(a, b):
    return lax.dot_general(a, b, (((0,), (0,)), ((), ())), preferred_element_type=F32)


def colsum(x):
    return jnp.sum(x, axis=0, keepdims=True)


def colmax(x):
    return jnp.max(x, axis=0, keepdims=True)


def kernel(
    n,
    q_h, k_h, v_h, g_h, seg_h,
    o_h, dq_h, dk_h, dv_h,
    q_all, k_all, v_all, g_all, seg_buf, flags,
    b_own, b_left, b_right, b_far,
    rp, rm, sendp, sendm, first,
    st_own, st_tot,
    acc_o, acc_dq, acc_dk, acc_dv, staged,
    in_loc, in_snd, in_rcv, seg_sem,
    e_snd, e_rcv, l_snd, l_rcv,
    out_snd, out_rcv,
):
    tok, feature = q_h.shape
    heads = HEADS // 2
    hd = feature // HEADS
    own = 2 * tok
    span = own - hd
    scale = math.log2(math.e) / math.sqrt(hd)
    inv_root = 1.0 / math.sqrt(hd)
    wide = 2 * hd

    def col(h, count=1):
        start = h * hd if isinstance(h, int) else pl.multiple_of(h * hd, hd)
        return pl.ds(start, count * hd)

    me = lax.axis_index("seq")
    core = lax.rem(me, 2)
    partner = me + 1 - 2 * core
    left = lax.rem(me + n - 2, n)
    right = lax.rem(me + 2, n)

    barrier = pltpu.get_barrier_semaphore()
    for peer in (partner, left, right):
        pl.semaphore_signal(barrier, inc=1, device_id={"seq": peer}, device_id_type=MESH)
    pl.semaphore_wait(barrier, 3)

    def remote(src, dst, snd, rcv, peer):
        return pltpu.make_async_remote_copy(
            src_ref=src, dst_ref=dst, send_sem=snd, recv_sem=rcv,
            device_id={"seq": peer}, device_id_type=MESH,
        )

    mine = pl.ds(pl.multiple_of(core * tok, tok), tok)
    theirs = pl.ds(pl.multiple_of((1 - core) * tok, tok), tok)
    pairs_in = ((k_h, k_all), (v_h, v_all), (q_h, q_all), (g_h, g_all))

    def group(which, s):
        return col(which * heads + s, 1 if s < DELAY else heads - DELAY)

    def in_local(j, s):
        src, dst = pairs_in[j]
        return pltpu.make_async_copy(src.at[:, group(core, s)], dst.at[mine, group(0, s)], in_loc.at[j, s])

    def in_remote(j, s):
        src, dst = pairs_in[j]
        return remote(
            src.at[:, group(1 - core, s)], dst.at[mine, group(0, s)], in_snd.at[j, s], in_rcv.at[j, s], partner
        )

    seg_local = pltpu.make_async_copy(seg_h, seg_buf.at[0, core], seg_sem.at[0])
    seg_remote = remote(seg_h, seg_buf.at[0, core], seg_sem.at[1], seg_sem.at[2], partner)
    seg_right = remote(seg_buf.at[0], seg_buf.at[1], seg_sem.at[3], seg_sem.at[4], right)
    seg_left = remote(seg_buf.at[0], seg_buf.at[2], seg_sem.at[5], seg_sem.at[6], left)
    for s in range(DELAY + 1):
        for j in range(4):
            in_remote(j, s).start()
            in_local(j, s).start()
        if s == 0:
            seg_local.start()
            seg_remote.start()

    tail, head, below = pl.ds(own - span, span), pl.ds(0, span), pl.ds(2 * span, STAT)

    def early(t, i):
        src, dst, peer = (
            (k_all.at[tail, col(t)], rp.at[t, pl.ds(0, span)], right),
            (q_all.at[head, col(t)], rm.at[t, pl.ds(0, span)], left),
            (v_all.at[tail, col(t)], rp.at[t, pl.ds(span, span)], right),
            (g_all.at[head, col(t)], rm.at[t, pl.ds(span, span)], left),
            (first.at[t], rm.at[t, below], left),
        )[i]
        return remote(src, dst, e_snd.at[t, i], e_rcv.at[t, i], peer)

    def to_right(h):
        return remote(sendp.at[h], rp.at[h + DELAY], l_snd.at[0, h], l_rcv.at[0, h], right)

    def to_left(h):
        return remote(sendm.at[h], rm.at[h + DELAY], l_snd.at[1, h], l_rcv.at[1, h], left)

    def start_early(t):
        for i, j in enumerate((0, 2, 1, 3)):
            in_local(j, t).wait()
            in_remote(j, t).wait_recv()
            early(t, i).start()

    start_early(0)
    seg_local.wait()
    seg_remote.wait_recv()
    seg_right.start()
    seg_left.start()

    def rows(ref, h, at, blocks):
        parts = [ref[h, at + b : at + b + 1, :] for b in range(blocks)]
        return parts[0] if blocks == 1 else jnp.concatenate(parts, axis=1)

    def put_rows(ref, h, at, value):
        for b in range(value.shape[1] // hd):
            ref[h, at + b : at + b + 1, :] = value[:, b * hd : (b + 1) * hd]

    def encode(lse, delta):
        out = []
        for row in lse:
            top = row.astype(BF16).astype(F32)
            mid = (row - top).astype(BF16).astype(F32)
            out += [top, mid, row - top - mid]
        for row in delta:
            top = row.astype(BF16).astype(F32)
            out += [top, row - top]
        out.append(jnp.zeros_like(out[0]))
        return jnp.concatenate(out, axis=0).astype(BF16)

    def decode(ref, t):
        table = ref[t, 2 * span : 2 * span + STAT, :].astype(F32)
        lse = [table[3 * b : 3 * b + 1] + table[3 * b + 1 : 3 * b + 2] + table[3 * b + 2 : 3 * b + 3] for b in range(3)]
        delta = [table[9 + 2 * b : 10 + 2 * b] + table[10 + 2 * b : 11 + 2 * b] for b in range(3)]
        return lse, delta

    def own_stats(h):
        lses, deltas = [], []
        for b in range(2):
            depth = (b + 1) * wide
            at = slice(b * wide, (b + 1) * wide)
            s = dot_nt(k_all[:depth, col(h)], q_all[at, col(h)]) * scale + b_own[:depth, at]
            dp = dot_nt(v_all[:depth, col(h)], g_all[at, col(h)])
            m = colmax(s)
            p = jnp.exp2(s - m)
            total = colsum(p)
            lse, delta = m + jnp.log2(total), colsum(p * dp) / total
            put_rows(st_own, h, 2 * b, lse)
            put_rows(st_own, h, 4 + 2 * b, delta)
            lses += [lse[:, :hd], lse[:, hd:]]
            deltas += [delta[:, :hd], delta[:, hd:]]
        return encode(lses[:3], deltas[:3])

    def finish(s, dp, lse, delta):
        p = jnp.exp2(s - lse)
        return p.astype(BF16), (p * ((dp - delta) * inv_root)).astype(BF16)

    def merge(lse, delta, parts):
        m = lse
        for s, _ in parts:
            m = jnp.maximum(m, colmax(s))
        first = jnp.exp2(lse - m)
        total, dn = first, delta * first
        probs = []
        for s, dp in parts:
            p = jnp.exp2(s - m)
            total = total + colsum(p)
            dn = dn + colsum(p * dp)
            probs.append(p)
        inv = 1.0 / total
        delta = dn * inv
        outs = []
        for p, (_, dp) in zip(probs, parts):
            p = p * inv
            outs.append((p.astype(BF16), (p * ((dp - delta) * inv_root)).astype(BF16)))
        return m + jnp.log2(total), delta, outs

    def cross(h):
        cut = span - wide
        nxt = jnp.minimum(h + DELAY, heads - 1)
        fresh = jnp.where(h + DELAY < heads, 1.0, 0.0)
        keys_right = jnp.broadcast_to((1.0 - flags[1:2, :]) * fresh, (span, hd)) > 0.5
        queries_left = jnp.broadcast_to(flags[0:1, :] * fresh, (span, hd)) > 0.5
        kl, vl = rp[h, :span], rp[h, span : 2 * span]
        lse_in, delta_in = decode(rm, h)
        k, v = k_all[:, col(h)], v_all[:, col(h)]
        qa, ga = rm[h, :wide], rm[h, span : span + wide]
        s1 = dot_nt(k, qa) * scale + b_right[:, :wide]
        s2 = dot_nt(kl[cut:], qa) * scale + b_far[...]
        d1, d2 = dot_nt(v, ga), dot_nt(vl[cut:], ga)
        lse, delta, ((p1, e1), (p2, e2)) = merge(
            jnp.concatenate(lse_in[:2], 1), jnp.concatenate(delta_in[:2], 1), ((s1, d1), (s2, d2))
        )
        lse_out, delta_out = [lse[:, :hd], lse[:, hd:]], [delta[:, :hd], delta[:, hd:]]
        dk, dv = dot_nn(e1, qa), dot_nn(p1, ga)
        dkl, dvl = dot_nn(e2, qa), dot_nn(p2, ga)
        for i, (a1, b1, a2, b2, kept) in enumerate(
            ((p1, v, p2, vl[cut:], k_all), (e1, k, e2, kl[cut:], v_all))
        ):
            part = dot_tn(a1, b1) + dot_tn(a2, b2)
            stay = kept[own - span : own - span + wide, col(nxt)].astype(F32)
            sendp[h, i * span : i * span + wide] = jnp.where(keys_right[:wide], stay, part).astype(BF16)
        qb, gb = rm[h, wide:span], rm[h, span + wide : 2 * span]
        s3 = dot_nt(k, qb) * scale + b_right[:, wide:]
        d3 = dot_nt(v, gb)
        lse, delta, ((p3, e3),) = merge(lse_in[2], delta_in[2], ((s3, d3),))
        sendp[h, 2 * span :] = encode(lse_out + [lse], delta_out + [delta])
        acc_dk[h] = dk + dot_nn(e3, qb)
        acc_dv[h] = dv + dot_nn(p3, gb)
        for i, (a3, b3, kept) in enumerate(((p3, v, k_all), (e3, k, v_all))):
            part = dot_tn(a3, b3)
            stay = kept[own - span + wide :, col(nxt)].astype(F32)
            sendp[h, i * span + wide : (i + 1) * span] = jnp.where(keys_right[wide:], stay, part).astype(BF16)
        to_right(h).start()
        dkl_sum = dvl_sum = None
        for b in range(2):
            at = slice(b * wide, (b + 1) * wide)
            q, g = q_all[at, col(h)], g_all[at, col(h)]
            s = dot_nt(kl, q) * scale + b_left[:, at]
            dp = dot_nt(vl, g)
            lse, delta, ((p, e),) = merge(
                rows(st_own, h, 2 * b, 2), rows(st_own, h, 4 + 2 * b, 2), ((s, dp),)
            )
            put_rows(st_tot, h, 2 * b, lse)
            put_rows(st_tot, h, 4 + 2 * b, delta)
            acc_o[h, at] = dot_tn(p, vl)
            acc_dq[h, at] = dot_tn(e, kl)
            dkb, dvb = dot_nn(e, q), dot_nn(p, g)
            dkl_sum = dkb if b == 0 else dkl_sum + dkb
            dvl_sum = dvb if b == 0 else dvl_sum + dvb
        for i, (total, extra, kept) in enumerate(((dkl_sum, dkl, q_all), (dvl_sum, dvl, g_all))):
            stay = kept[:span, col(nxt)].astype(F32)
            sendm[h, i * span : i * span + cut] = jnp.where(queries_left[:cut], stay[:cut], total[:cut]).astype(BF16)
            sendm[h, i * span + cut : (i + 1) * span] = jnp.where(
                queries_left[cut:], stay[cut:], total[cut:] + extra
            ).astype(BF16)

    def close(h):
        t = h + DELAY
        asked = flags[0:1, :] > 0.5
        back = jnp.broadcast_to(flags[0:1, :], (span, hd)) > 0.5
        back_keys = jnp.broadcast_to(1.0 - flags[1:2, :], (span, hd)) > 0.5
        lse = [st_tot[h, b : b + 1, :] for b in range(4)]
        delta = [st_tot[h, 4 + b : 5 + b, :] for b in range(4)]
        lse_back, delta_back = decode(rp, t)
        for b in range(3):
            lse[b] = jnp.where(asked, lse_back[b], lse[b])
            delta[b] = jnp.where(asked, delta_back[b], delta[b])
        add = [jnp.where(back, rp[t, i * span : (i + 1) * span].astype(F32), 0.0) for i in range(2)]
        for b in range(2):
            depth = (b + 1) * wide
            at = slice(b * wide, (b + 1) * wide)
            q, g = q_all[at, col(h)], g_all[at, col(h)]
            k, v = k_all[:depth, col(h)], v_all[:depth, col(h)]
            s = dot_nt(k, q) * scale + b_own[:depth, at]
            dp = dot_nt(v, g)
            p, e = finish(
                s, dp, jnp.concatenate(lse[2 * b : 2 * b + 2], 1), jnp.concatenate(delta[2 * b : 2 * b + 2], 1)
            )
            acc_dk[h, :depth] += dot_nn(e, q)
            acc_dv[h, :depth] += dot_nn(p, g)
            for i, (value, acc) in enumerate(((dot_tn(p, v), acc_o), (dot_tn(e, k), acc_dq))):
                value = value + acc[h, at]
                if b == 0:
                    staged[h, i, at] = (value + add[i][:wide]).astype(BF16)
                else:
                    staged[h, i, wide:span] = (value[: span - wide] + add[i][wide:]).astype(BF16)
                    staged[h, i, span:] = value[span - wide :].astype(BF16)
        for i, acc in ((0, acc_dk), (1, acc_dv)):
            staged[h, 2 + i, : own - span] = acc[h, : own - span].astype(BF16)
            staged[h, 2 + i, own - span :] = (
                acc[h, own - span :] + jnp.where(back_keys, rm[t, i * span : (i + 1) * span].astype(F32), 0.0)
            ).astype(BF16)

    outs = (o_h, dq_h, dk_h, dv_h)

    def out_remote(j, h):
        return remote(
            staged.at[h, j, theirs], outs[j].at[:, col(core * heads + h)],
            out_snd.at[j, h], out_rcv.at[j, h], partner,
        )

    def seg_row(chip, b):
        return seg_buf[chip, b // 2, b % 2 : b % 2 + 1, :].astype(F32)

    def as_column(row):
        return jnp.transpose(jnp.broadcast_to(row, (hd, hd)))

    def tile(a, b):
        return slice(a * hd, (a + 1) * hd), slice(b * hd, (b + 1) * hd)

    own_rows = [seg_row(0, b) for b in range(4)]
    own_cols = [as_column(row) for row in own_rows]
    causal = lax.broadcasted_iota(jnp.int32, (hd, hd), 0) <= lax.broadcasted_iota(jnp.int32, (hd, hd), 1)
    for a in range(4):
        for b in range(4):
            same = own_cols[a] == own_rows[b]
            if a > b:
                b_own[tile(a, b)] = jnp.full((hd, hd), NEG, F32)
            else:
                b_own[tile(a, b)] = jnp.where(same & causal if a == b else same, 0.0, NEG)

    first[0] = own_stats(0)
    early(0, 4).start()
    for t in range(1, DELAY):
        start_early(t)
        first[t] = own_stats(t)
        early(t, 4).start()

    seg_right.wait_recv()
    seg_left.wait_recv()

    def seg_at(chip, b, lane):
        return jnp.broadcast_to(seg_row(chip, b)[:, lane : lane + 1], (1, hd))

    asks_left = seg_at(1, 0, hd - 1) == seg_at(0, 0, 0)
    asks_right = seg_at(0, 0, hd - 1) == seg_at(2, 0, 0)
    flags[0:1, :] = jnp.where(asks_left, 1.0, 0.0)
    flags[1:2, :] = jnp.where(asks_right, 1.0, 0.0)
    left_cols = [as_column(jnp.where(asks_left, -1.0, seg_row(1, b + 1))) for b in range(3)]
    right_rows = [jnp.where(asks_right, seg_row(2, b), -2.0) for b in range(3)]
    for a in range(4):
        for b in range(4):
            if a < 3:
                b_left[tile(a, b)] = jnp.where(left_cols[a] == own_rows[b], 0.0, NEG)
            if b < 3:
                b_right[tile(a, b)] = jnp.where(own_cols[a] == right_rows[b], 0.0, NEG)
            if a < 2 and b < 2:
                b_far[tile(a, b)] = jnp.where(left_cols[a + 1] == right_rows[b], 0.0, NEG)

    def step(i, _):
        @pl.when(i == 0)
        def _():
            for j in range(4):
                in_local(j, DELAY).wait()
                in_remote(j, DELAY).wait_recv()

        @pl.when(i + DELAY < heads)
        def _():
            sendm[i, 2 * span :] = own_stats(i + DELAY)

        @pl.when(i >= heads - DELAY)
        def _():
            @pl.when(i < heads)
            def _():
                sendm[i, 2 * span :] = jnp.zeros((STAT, hd), BF16)

        @pl.when(i < DELAY)
        def _():
            for j in range(5):
                early(i, j).wait()

        @pl.when(i >= DELAY)
        def _():
            to_right(i - DELAY).wait()
            to_left(i - DELAY).wait()

        @pl.when(i < heads)
        def _():
            cross(i)
            to_left(i).start()

        @pl.when(i >= DELAY)
        def _():
            h = i - DELAY
            close(h)
            for j in range(4):
                out_remote(j, h).start()
            for j in range(4):
                outs[j][:, col(core * heads + h)] = staged[h, j, mine, :]

        @pl.when(i > DELAY)
        def _():
            for j in range(4):
                out_remote(j, i - DELAY - 1).wait()

        return 0

    lax.fori_loop(0, heads + DELAY, step, 0)
    for s in range(DELAY + 1):
        for j in range(4):
            in_remote(j, s).wait_send()
    for j in range(4):
        out_remote(j, heads - 1).wait()
    seg_remote.wait_send()
    seg_right.wait_send()
    seg_left.wait_send()


def store(*refs):
    sem = refs[8]
    copies = [pltpu.make_async_copy(refs[j], refs[4 + j], sem.at[j]) for j in range(4)]
    for copy in copies:
        copy.start()
    for copy in copies:
        copy.wait()


def local(n, queries, keys, values, out_grad, segments):
    tok, feature = queries.shape
    heads, hd = HEADS // 2, feature // HEADS
    own = 2 * tok
    span = own - hd
    slots = heads + DELAY
    rows = 2 * span + STAT
    out = jax.ShapeDtypeStruct((tok, feature), BF16)
    dma = pltpu.SemaphoreType.DMA
    vm = pltpu.VMEM
    results = pl.pallas_call(
        functools.partial(kernel, n),
        out_shape=(vm((tok, feature), BF16),) * 4,
        in_specs=[pl.BlockSpec(memory_space=pltpu.HBM)] * 5,
        out_specs=[pl.BlockSpec(memory_space=vm)] * 4,
        scratch_shapes=[
            vm((own, heads * hd), BF16), vm((own, heads * hd), BF16),
            vm((own, heads * hd), BF16), vm((own, heads * hd), BF16),
            vm((3, 2, 2, hd), jnp.int32), vm((8, hd), F32),
            vm((own, own), F32), vm((span, own), F32), vm((own, span), F32), vm((2 * hd, 2 * hd), F32),
            vm((slots, rows, hd), BF16), vm((slots, rows, hd), BF16),
            vm((heads, rows, hd), BF16), vm((heads, rows, hd), BF16), vm((DELAY, STAT, hd), BF16),
            vm((heads, 8, hd), F32), vm((heads, 8, hd), F32),
            vm((heads, own, hd), F32), vm((heads, own, hd), F32),
            vm((heads, own, hd), F32), vm((heads, own, hd), F32),
            vm((heads, 4, own, hd), BF16),
            dma((4, DELAY + 1)), dma((4, DELAY + 1)), dma((4, DELAY + 1)), dma((7,)),
            dma((DELAY, 5)), dma((DELAY, 5)), dma((2, heads)), dma((2, heads)),
            dma((4, heads)), dma((4, heads)),
        ],
        compiler_params=pltpu.CompilerParams(
            collective_id=0, has_side_effects=True, vmem_limit_bytes=51 * 2**20
        ),
        name="packed_attention",
    )(*(pltpu.with_memory_space_constraint(x, pltpu.HBM) for x in (queries, keys, values, out_grad)), segments.reshape(2, tok // 2))
    return pl.pallas_call(
        store,
        out_shape=(out,) * 4,
        in_specs=[pl.BlockSpec(memory_space=pl.ANY)] * 4,
        out_specs=[pl.BlockSpec(memory_space=pl.ANY)] * 4,
        scratch_shapes=[dma((4,))],
        compiler_params=pltpu.CompilerParams(vmem_limit_bytes=2**20),
        name="store_results",
    )(*(pltpu.with_memory_space_constraint(r, vm) for r in results))


def solution(mesh):
    spec = P(("branch", "seq"), None)
    return jax.shard_map(
        functools.partial(local, mesh.shape["seq"]),
        mesh=mesh,
        in_specs=(spec,) * 4 + (P(("branch", "seq")),),
        out_specs=(spec,) * 4,
        check_vma=False,
    )
```

time: 93.9 us -> 79.2 us (0.84)
  Pallas kernels: 86.4 us -> 78.5 us
  local copies, waits for them, and re-layouts: 6.57 us -> 0 us
    pallas_call x1 -> x2, Pallas kernels: 86.4 us -> 78.5 us  [the longest x1 76.4 us: local(): pl.pallas_call(functools.partial(kernel, n), out_shape=(vm((tok, feature)...]
    unnamed x10 -> x0, local copies, waits for them, and re-layouts: 6.57 us -> none
where the time goes in v2:
time: 79.2 us; the launch traced here: 79.1 us
  Pallas kernels  78.5 us (99%)
    pallas_call x1, Pallas kernels, local(): pl.pallas_call(functools.partial(kernel, n), out_shape=(vm((tok, feature)...  76.4 us
    pallas_call x1, Pallas kernels, local(): pl.pallas_call(store, out_shape=(out,) * 4, in_specs=[pl.BlockSpec(memory...  2.04 us

profile of v2, /device:TPU:37, one launch (start us, length us, event | category | flops | bytes accessed | tf_op | source)
XLA Modules:
  0.0 79.1 jit_solution(11644599825709830350)
XLA Ops:
  0.6 76.4 %packed_attention.1 = (bf16[256,2048]{1,0:T(8,128)(2,1)S(1)}, bf16[256,2048]{1,0:T(8,128)(2,1)S(1)}, bf16[256,2048]{1,0:T(8,128)(2,1)S(1)}, bf16[256,2048]{1,0:T(8,128)(2,1)S(1)}) custom-call(bf16[256,2048]{1,0:T(8,128)(2,1)} %q_h.1, bf16[256,2048]{1,0:T(8,128)(2,1)} %k_h.1, bf16[256,2048]{1,0:T(8,128)(2,1)} %v_h.1, bf16[256,2048]{1,0:T(8,128)(2,1)} %g_h.1, ...), custom_call_target="tpu_custom_call" | custom-call | tf_op jit(solution)/shard_map/packed_attention/pallas_call | solution.py:440
  77.1 2.0 %store_results.1 = (bf16[256,2048]{1,0:T(8,128)(2,1)}, bf16[256,2048]{1,0:T(8,128)(2,1)}, bf16[256,2048]{1,0:T(8,128)(2,1)}, bf16[256,2048]{1,0:T(8,128)(2,1)}) custom-call(bf16[256,2048]{1,0:T(8,128)(2,1)S(1)} %get-tuple-element.8.refs_0_, bf16[256,2048]{1,0:T(8,128)(2,1)S(1)} %get-tuple-element.9.refs_1_, bf16[256,2048]{1,0:T(8,128)(2,1)S(1)} %get-tuple-element.10.refs_2_, ...), custom_call_target="tpu_custom_call" | custom-call | tf_op jit(solution)/shard_map/store_results/pallas_call | solution.py:465

commit v3 on v2

--- a/solution.py
+++ b/solution.py
@@ -47,7 +47,7 @@
     st_own, st_tot,
     acc_o, acc_dq, acc_dk, acc_dv, staged,
     in_loc, in_snd, in_rcv, seg_sem,
-    e_snd, e_rcv, l_snd, l_rcv,
+    r_snd, r_rcv, e_snd, e_rcv, l_snd, l_rcv, ready,
     out_snd, out_rcv,
 ):
     tok, feature = q_h.shape
@@ -66,13 +66,25 @@
     me = lax.axis_index("seq")
     core = lax.rem(me, 2)
     partner = me + 1 - 2 * core
+    chip = lax.div(me, 2)
     left = lax.rem(me + n - 2, n)
     right = lax.rem(me + 2, n)
+    has_left = chip > 0
+    has_right = chip < n // 2 - 1
 
     barrier = pltpu.get_barrier_semaphore()
-    for peer in (partner, left, right):
-        pl.semaphore_signal(barrier, inc=1, device_id={"seq": peer}, device_id_type=MESH)
-    pl.semaphore_wait(barrier, 3)
+
+    def signal(sem, peer):
+        pl.semaphore_signal(sem, inc=1, device_id={"seq": peer}, device_id_type=MESH)
+
+    @pl.when(has_left)
+    def _():
+        for c in range(2):
+            signal(barrier, 2 * lax.div(left, 2) + c)
+
+    @pl.when((core == 1) | jnp.logical_not(has_right))
+    def _():
+        signal(barrier, partner)
 
     def remote(src, dst, snd, rcv, peer):
         return pltpu.make_async_remote_copy(
@@ -103,23 +115,38 @@
     seg_left = remote(seg_buf.at[0], seg_buf.at[2], seg_sem.at[5], seg_sem.at[6], left)
     for s in range(DELAY + 1):
         for j in range(4):
-            in_remote(j, s).start()
             in_local(j, s).start()
-        if s == 0:
-            seg_local.start()
-            seg_remote.start()
-
-    tail, head, below = pl.ds(own - span, span), pl.ds(0, span), pl.ds(2 * span, STAT)
-
-    def early(t, i):
-        src, dst, peer = (
-            (k_all.at[tail, col(t)], rp.at[t, pl.ds(0, span)], right),
-            (q_all.at[head, col(t)], rm.at[t, pl.ds(0, span)], left),
-            (v_all.at[tail, col(t)], rp.at[t, pl.ds(span, span)], right),
-            (g_all.at[head, col(t)], rm.at[t, pl.ds(span, span)], left),
-            (first.at[t], rm.at[t, below], left),
+    seg_local.start()
+    pl.semaphore_wait(barrier, jnp.where(has_right, 3 - core, 1))
+
+    @pl.when(has_right)
+    def _():
+        signal(ready.at[0], right)
+
+    @pl.when(core == 0)
+    def _():
+        signal(ready.at[1], partner)
+
+    head, below = pl.ds(0, span), pl.ds(2 * span, STAT)
+
+    def early_left(t, i):
+        src, dst = (
+            (q_all.at[head, col(t)], rm.at[t, pl.ds(0, span)]),
+            (g_all.at[head, col(t)], rm.at[t, pl.ds(span, span)]),
+            (first.at[t], rm.at[t, below]),
         )[i]
-        return remote(src, dst, e_snd.at[t, i], e_rcv.at[t, i], peer)
+        return remote(src, dst, e_snd.at[t, i], e_rcv.at[t, i], left)
+
+    skip = own - span
+
+    def early_right(t, i, source, target):
+        count = tok - skip if source == 0 else tok
+        at = i * span if source == 0 else i * span + tok - skip
+        rows = pl.ds(skip, count) if source == 0 else pl.ds(0, count)
+        return remote(
+            pairs_in[i][0].at[rows, col(target * heads + t)], rp.at[t, pl.ds(at, count)],
+            r_snd.at[t, i, target], r_rcv.at[t, i, source], 2 * lax.div(right, 2) + target,
+        )
 
     def to_right(h):
         return remote(sendp.at[h], rp.at[h + DELAY], l_snd.at[0, h], l_rcv.at[0, h], right)
@@ -127,17 +154,50 @@
     def to_left(h):
         return remote(sendm.at[h], rm.at[h + DELAY], l_snd.at[1, h], l_rcv.at[1, h], left)
 
-    def start_early(t):
-        for i, j in enumerate((0, 2, 1, 3)):
-            in_local(j, t).wait()
-            in_remote(j, t).wait_recv()
-            early(t, i).start()
-
-    start_early(0)
+    for source in range(2):
+
+        @pl.when(has_right & (core == source))
+        def _():
+            for t in range(DELAY):
+                for target in range(2):
+                    for i in range(2):
+                        early_right(t, i, source, target).start()
+
+    @pl.when(core == 1)
+    def _():
+        pl.semaphore_wait(ready.at[1], 1)
+
+    seg_remote.start()
+    for s in range(DELAY + 1):
+        for j in range(4):
+            in_remote(j, s).start()
+
+    @pl.when(jnp.logical_not(has_left))
+    def _():
+        seg_buf[1] = jnp.full(seg_buf.shape[1:], -1, jnp.int32)
+
+        def clear(t, _):
+            rp[t] = jnp.zeros(rp.shape[1:], BF16)
+            return 0
+
+        lax.fori_loop(0, rp.shape[0], clear, 0)
+
+    @pl.when(jnp.logical_not(has_right))
+    def _():
+        seg_buf[2] = jnp.full(seg_buf.shape[1:], -3, jnp.int32)
+
+        def clear(t, _):
+            rm[t] = jnp.zeros(rm.shape[1:], BF16)
+            return 0
+
+        lax.fori_loop(0, rm.shape[0], clear, 0)
+
     seg_local.wait()
     seg_remote.wait_recv()
-    seg_right.start()
-    seg_left.start()
+
+    @pl.when(has_right)
+    def _():
+        seg_right.start()
 
     def rows(ref, h, at, blocks):
         parts = [ref[h, at + b : at + b + 1, :] for b in range(blocks)]
@@ -242,7 +302,11 @@
             part = dot_tn(a3, b3)
             stay = kept[own - span + wide :, col(nxt)].astype(F32)
             sendp[h, i * span + wide : (i + 1) * span] = jnp.where(keys_right[wide:], stay, part).astype(BF16)
-        to_right(h).start()
+
+        @pl.when(has_right)
+        def _():
+            to_right(h).start()
+
         dkl_sum = dvl_sum = None
         for b in range(2):
             at = slice(b * wide, (b + 1) * wide)
@@ -331,15 +395,25 @@
             else:
                 b_own[tile(a, b)] = jnp.where(same & causal if a == b else same, 0.0, NEG)
 
-    first[0] = own_stats(0)
-    early(0, 4).start()
-    for t in range(1, DELAY):
-        start_early(t)
+    for t in range(DELAY):
+        for j in range(4):
+            in_local(j, t).wait()
+            in_remote(j, t).wait_recv()
         first[t] = own_stats(t)
-        early(t, 4).start()
-
-    seg_right.wait_recv()
-    seg_left.wait_recv()
+
+    @pl.when(has_left)
+    def _():
+        pl.semaphore_wait(ready.at[0], 1)
+        for t in range(DELAY):
+            for i in range(3):
+                early_left(t, i).start()
+            if t == 0:
+                seg_left.start()
+        seg_right.wait_recv()
+
+    @pl.when(has_right)
+    def _():
+        seg_left.wait_recv()
 
     def seg_at(chip, b, lane):
         return jnp.broadcast_to(seg_row(chip, b)[:, lane : lane + 1], (1, hd))
@@ -376,20 +450,36 @@
             def _():
                 sendm[i, 2 * span :] = jnp.zeros((STAT, hd), BF16)
 
-        @pl.when(i < DELAY)
-        def _():
-            for j in range(5):
-                early(i, j).wait()
-
-        @pl.when(i >= DELAY)
-        def _():
-            to_right(i - DELAY).wait()
-            to_left(i - DELAY).wait()
+        @pl.when((i < DELAY) & has_left)
+        def _():
+            for j in range(2):
+                for source in range(2):
+                    early_right(i, j, source, 0).wait_recv()
+            for j in range(3):
+                early_left(i, j).wait_send()
+
+        @pl.when((i < DELAY) & has_right)
+        def _():
+            for j in range(3):
+                early_left(i, j).wait_recv()
+
+        @pl.when((i >= DELAY) & has_left)
+        def _():
+            to_right(i - DELAY).wait_recv()
+            to_left(i - DELAY).wait_send()
+
+        @pl.when((i >= DELAY) & has_right)
+        def _():
+            to_left(i - DELAY).wait_recv()
+            to_right(i - DELAY).wait_send()
 
         @pl.when(i < heads)
         def _():
             cross(i)
-            to_left(i).start()
+
+            @pl.when(has_left)
+            def _():
+                to_left(i).start()
 
         @pl.when(i >= DELAY)
         def _():
@@ -414,8 +504,23 @@
     for j in range(4):
         out_remote(j, heads - 1).wait()
     seg_remote.wait_send()
-    seg_right.wait_send()
-    seg_left.wait_send()
+
+    for source in range(2):
+
+        @pl.when(has_right & (core == source))
+        def _():
+            for t in range(DELAY):
+                for target in range(2):
+                    for i in range(2):
+                        early_right(t, i, source, target).wait_send()
+
+    @pl.when(has_right)
+    def _():
+        seg_right.wait_send()
+
+    @pl.when(has_left)
+    def _():
+        seg_left.wait_send()
 
 
 def store(*refs):
@@ -454,7 +559,8 @@
             vm((heads, own, hd), F32), vm((heads, own, hd), F32),
             vm((heads, 4, own, hd), BF16),
             dma((4, DELAY + 1)), dma((4, DELAY + 1)), dma((4, DELAY + 1)), dma((7,)),
-            dma((DELAY, 5)), dma((DELAY, 5)), dma((2, heads)), dma((2, heads)),
+            dma((DELAY, 2, 2)), dma((DELAY, 2, 2)), dma((DELAY, 3)), dma((DELAY, 3)),
+            dma((2, heads)), dma((2, heads)), pltpu.SemaphoreType.REGULAR((2,)),
             dma((4, heads)), dma((4, heads)),
         ],
         compiler_params=pltpu.CompilerParams(

time: 79.2 us -> 72.1 us (0.910)
  Pallas kernels: 78.5 us -> 71.3 us
    pallas_call x1, Pallas kernels: 76.4 us -> 69.3 us  [local(): pl.pallas_call(functools.partial(kernel, n), out_shape=(vm((tok, feature)...]
where the time goes in v3:
time: 72.1 us; the launch traced here: 72 us
  Pallas kernels  71.3 us (99%)
    pallas_call x1, Pallas kernels, local(): pl.pallas_call(functools.partial(kernel, n), out_shape=(vm((tok, feature)...  69.3 us
    pallas_call x1, Pallas kernels, local(): pl.pallas_call(store, out_shape=(out,) * 4, in_specs=[pl.BlockSpec(memory...  2.04 us

profile of v3, /device:TPU:37, one launch (start us, length us, event | category | flops | bytes accessed | tf_op | source)
XLA Modules:
  0.0 72.0 jit_solution(959656002377279846)
XLA Ops:
  0.6 69.3 %packed_attention.1 = (bf16[256,2048]{1,0:T(8,128)(2,1)S(1)}, bf16[256,2048]{1,0:T(8,128)(2,1)S(1)}, bf16[256,2048]{1,0:T(8,128)(2,1)S(1)}, bf16[256,2048]{1,0:T(8,128)(2,1)S(1)}) custom-call(bf16[256,2048]{1,0:T(8,128)(2,1)} %q_h.1, bf16[256,2048]{1,0:T(8,128)(2,1)} %k_h.1, bf16[256,2048]{1,0:T(8,128)(2,1)} %v_h.1, bf16[256,2048]{1,0:T(8,128)(2,1)} %g_h.1, ...), custom_call_target="tpu_custom_call" | custom-call | tf_op jit(solution)/shard_map/packed_attention/pallas_call | solution.py:545
  69.9 2.0 %store_results.1 = (bf16[256,2048]{1,0:T(8,128)(2,1)}, bf16[256,2048]{1,0:T(8,128)(2,1)}, bf16[256,2048]{1,0:T(8,128)(2,1)}, bf16[256,2048]{1,0:T(8,128)(2,1)}) custom-call(bf16[256,2048]{1,0:T(8,128)(2,1)S(1)} %get-tuple-element.8.refs_0_, bf16[256,2048]{1,0:T(8,128)(2,1)S(1)} %get-tuple-element.9.refs_1_, bf16[256,2048]{1,0:T(8,128)(2,1)S(1)} %get-tuple-element.10.refs_2_, ...), custom_call_target="tpu_custom_call" | custom-call | tf_op jit(solution)/shard_map/store_results/pallas_call | solution.py:571

commit v4 on v3

--- a/solution.py
+++ b/solution.py
@@ -44,7 +44,7 @@
     q_all, k_all, v_all, g_all, seg_buf, flags,
     b_own, b_left, b_right, b_far,
     rp, rm, sendp, sendm, first,
-    st_own, st_tot,
+    st_own, st_tot, st_max, probs, dprobs,
     acc_o, acc_dq, acc_dk, acc_dv, staged,
     in_loc, in_snd, in_rcv, seg_sem,
     r_snd, r_rcv, e_snd, e_rcv, l_snd, l_rcv, ready,
@@ -113,10 +113,6 @@
     seg_remote = remote(seg_h, seg_buf.at[0, core], seg_sem.at[1], seg_sem.at[2], partner)
     seg_right = remote(seg_buf.at[0], seg_buf.at[1], seg_sem.at[3], seg_sem.at[4], right)
     seg_left = remote(seg_buf.at[0], seg_buf.at[2], seg_sem.at[5], seg_sem.at[6], left)
-    for s in range(DELAY + 1):
-        for j in range(4):
-            in_local(j, s).start()
-    seg_local.start()
     pl.semaphore_wait(barrier, jnp.where(has_right, 3 - core, 1))
 
     @pl.when(has_right)
@@ -168,9 +164,11 @@
         pl.semaphore_wait(ready.at[1], 1)
 
     seg_remote.start()
+    seg_local.start()
     for s in range(DELAY + 1):
         for j in range(4):
             in_remote(j, s).start()
+            in_local(j, s).start()
 
     @pl.when(jnp.logical_not(has_left))
     def _():
@@ -235,16 +233,15 @@
             m = colmax(s)
             p = jnp.exp2(s - m)
             total = colsum(p)
+            kept = slice(b * wide, b * wide + depth)
+            probs[h, kept], dprobs[h, kept] = p, dp
+            put_rows(st_max, h, 2 * b, m)
             lse, delta = m + jnp.log2(total), colsum(p * dp) / total
             put_rows(st_own, h, 2 * b, lse)
             put_rows(st_own, h, 4 + 2 * b, delta)
             lses += [lse[:, :hd], lse[:, hd:]]
             deltas += [delta[:, :hd], delta[:, hd:]]
         return encode(lses[:3], deltas[:3])
-
-    def finish(s, dp, lse, delta):
-        p = jnp.exp2(s - lse)
-        return p.astype(BF16), (p * ((dp - delta) * inv_root)).astype(BF16)
 
     def merge(lse, delta, parts):
         m = lse
@@ -283,8 +280,6 @@
             jnp.concatenate(lse_in[:2], 1), jnp.concatenate(delta_in[:2], 1), ((s1, d1), (s2, d2))
         )
         lse_out, delta_out = [lse[:, :hd], lse[:, hd:]], [delta[:, :hd], delta[:, hd:]]
-        dk, dv = dot_nn(e1, qa), dot_nn(p1, ga)
-        dkl, dvl = dot_nn(e2, qa), dot_nn(p2, ga)
         for i, (a1, b1, a2, b2, kept) in enumerate(
             ((p1, v, p2, vl[cut:], k_all), (e1, k, e2, kl[cut:], v_all))
         ):
@@ -296,8 +291,6 @@
         d3 = dot_nt(v, gb)
         lse, delta, ((p3, e3),) = merge(lse_in[2], delta_in[2], ((s3, d3),))
         sendp[h, 2 * span :] = encode(lse_out + [lse], delta_out + [delta])
-        acc_dk[h] = dk + dot_nn(e3, qb)
-        acc_dv[h] = dv + dot_nn(p3, gb)
         for i, (a3, b3, kept) in enumerate(((p3, v, k_all), (e3, k, v_all))):
             part = dot_tn(a3, b3)
             stay = kept[own - span + wide :, col(nxt)].astype(F32)
@@ -308,6 +301,8 @@
             to_right(h).start()
 
         dkl_sum = dvl_sum = None
+        dkl, dvl = dot_nn(e2, qa), dot_nn(p2, ga)
+        stay_here = []
         for b in range(2):
             at = slice(b * wide, (b + 1) * wide)
             q, g = q_all[at, col(h)], g_all[at, col(h)]
@@ -318,8 +313,7 @@
             )
             put_rows(st_tot, h, 2 * b, lse)
             put_rows(st_tot, h, 4 + 2 * b, delta)
-            acc_o[h, at] = dot_tn(p, vl)
-            acc_dq[h, at] = dot_tn(e, kl)
+            stay_here.append((at, p, e))
             dkb, dvb = dot_nn(e, q), dot_nn(p, g)
             dkl_sum = dkb if b == 0 else dkl_sum + dkb
             dvl_sum = dvb if b == 0 else dvl_sum + dvb
@@ -329,6 +323,16 @@
             sendm[h, i * span + cut : (i + 1) * span] = jnp.where(
                 queries_left[cut:], stay[cut:], total[cut:] + extra
             ).astype(BF16)
+
+        @pl.when(has_left)
+        def _():
+            to_left(h).start()
+
+        acc_dk[h] = dot_nn(e1, qa) + dot_nn(e3, qb)
+        acc_dv[h] = dot_nn(p1, ga) + dot_nn(p3, gb)
+        for at, p, e in stay_here:
+            acc_o[h, at] = dot_tn(p, vl)
+            acc_dq[h, at] = dot_tn(e, kl)
 
     def close(h):
         t = h + DELAY
@@ -347,11 +351,11 @@
             at = slice(b * wide, (b + 1) * wide)
             q, g = q_all[at, col(h)], g_all[at, col(h)]
             k, v = k_all[:depth, col(h)], v_all[:depth, col(h)]
-            s = dot_nt(k, q) * scale + b_own[:depth, at]
-            dp = dot_nt(v, g)
-            p, e = finish(
-                s, dp, jnp.concatenate(lse[2 * b : 2 * b + 2], 1), jnp.concatenate(delta[2 * b : 2 * b + 2], 1)
-            )
+            kept = slice(b * wide, b * wide + depth)
+            shrink = jnp.exp2(rows(st_max, h, 2 * b, 2) - jnp.concatenate(lse[2 * b : 2 * b + 2], 1))
+            p = probs[h, kept] * shrink
+            e = (p * ((dprobs[h, kept] - jnp.concatenate(delta[2 * b : 2 * b + 2], 1)) * inv_root)).astype(BF16)
+            p = p.astype(BF16)
             acc_dk[h, :depth] += dot_nn(e, q)
             acc_dv[h, :depth] += dot_nn(p, g)
             for i, (value, acc) in enumerate(((dot_tn(p, v), acc_o), (dot_tn(e, k), acc_dq))):
@@ -361,6 +365,8 @@
                 else:
                     staged[h, i, wide:span] = (value[: span - wide] + add[i][wide:]).astype(BF16)
                     staged[h, i, span:] = value[span - wide :].astype(BF16)
+        for j in range(2):
+            out_remote(j, h).start()
         for i, acc in ((0, acc_dk), (1, acc_dv)):
             staged[h, 2 + i, : own - span] = acc[h, : own - span].astype(BF16)
             staged[h, 2 + i, own - span :] = (
@@ -477,15 +483,11 @@
         def _():
             cross(i)
 
-            @pl.when(has_left)
-            def _():
-                to_left(i).start()
-
         @pl.when(i >= DELAY)
         def _():
             h = i - DELAY
             close(h)
-            for j in range(4):
+            for j in range(2, 4):
                 out_remote(j, h).start()
             for j in range(4):
                 outs[j][:, col(core * heads + h)] = staged[h, j, mine, :]
@@ -554,7 +556,8 @@
             vm((own, own), F32), vm((span, own), F32), vm((own, span), F32), vm((2 * hd, 2 * hd), F32),
             vm((slots, rows, hd), BF16), vm((slots, rows, hd), BF16),
             vm((heads, rows, hd), BF16), vm((heads, rows, hd), BF16), vm((DELAY, STAT, hd), BF16),
-            vm((heads, 8, hd), F32), vm((heads, 8, hd), F32),
+            vm((heads, 8, hd), F32), vm((heads, 8, hd), F32), vm((heads, 8, hd), F32),
+            vm((heads, 6 * hd, 2 * hd), F32), vm((heads, 6 * hd, 2 * hd), F32),
             vm((heads, own, hd), F32), vm((heads, own, hd), F32),
             vm((heads, own, hd), F32), vm((heads, own, hd), F32),
             vm((heads, 4, own, hd), BF16),

time: 72.1 us -> 70.4 us (0.976)
  Pallas kernels: 71.3 us -> 69.6 us
    pallas_call x1, Pallas kernels: 69.3 us -> 67.6 us  [local(): pl.pallas_call(functools.partial(kernel, n), out_shape=(vm((tok, feature)...]
where the time goes in v4:
time: 70.4 us; the launch traced here: 70.2 us
  Pallas kernels  69.6 us (99%)
    pallas_call x1, Pallas kernels, local(): pl.pallas_call(functools.partial(kernel, n), out_shape=(vm((tok, feature)...  67.6 us
    pallas_call x1, Pallas kernels, local(): pl.pallas_call(store, out_shape=(out,) * 4, in_specs=[pl.BlockSpec(memory...  2.04 us

profile of v4, /device:TPU:37, one launch (start us, length us, event | category | flops | bytes accessed | tf_op | source)
XLA Modules:
  0.0 70.2 jit_solution(13956686083098366255)
XLA Ops:
  0.6 67.6 %packed_attention.1 = (bf16[256,2048]{1,0:T(8,128)(2,1)S(1)}, bf16[256,2048]{1,0:T(8,128)(2,1)S(1)}, bf16[256,2048]{1,0:T(8,128)(2,1)S(1)}, bf16[256,2048]{1,0:T(8,128)(2,1)S(1)}) custom-call(bf16[256,2048]{1,0:T(8,128)(2,1)} %q_h.1, bf16[256,2048]{1,0:T(8,128)(2,1)} %k_h.1, bf16[256,2048]{1,0:T(8,128)(2,1)} %v_h.1, bf16[256,2048]{1,0:T(8,128)(2,1)} %g_h.1, ...), custom_call_target="tpu_custom_call" | custom-call | tf_op jit(solution)/shard_map/packed_attention/pallas_call | solution.py:547
  68.2 2.0 %store_results.1 = (bf16[256,2048]{1,0:T(8,128)(2,1)}, bf16[256,2048]{1,0:T(8,128)(2,1)}, bf16[256,2048]{1,0:T(8,128)(2,1)}, bf16[256,2048]{1,0:T(8,128)(2,1)}) custom-call(bf16[256,2048]{1,0:T(8,128)(2,1)S(1)} %get-tuple-element.8.refs_0_, bf16[256,2048]{1,0:T(8,128)(2,1)S(1)} %get-tuple-element.9.refs_1_, bf16[256,2048]{1,0:T(8,128)(2,1)S(1)} %get-tuple-element.10.refs_2_, ...), custom_call_target="tpu_custom_call" | custom-call | tf_op jit(solution)/shard_map/store_results/pallas_call | solution.py:574

commit v5 on v4

--- a/solution.py
+++ b/solution.py
@@ -111,7 +111,13 @@
 
     seg_local = pltpu.make_async_copy(seg_h, seg_buf.at[0, core], seg_sem.at[0])
     seg_remote = remote(seg_h, seg_buf.at[0, core], seg_sem.at[1], seg_sem.at[2], partner)
-    seg_right = remote(seg_buf.at[0], seg_buf.at[1], seg_sem.at[3], seg_sem.at[4], right)
+
+    def seg_right(source, target):
+        return remote(
+            seg_h, seg_buf.at[1, source], seg_sem.at[3 + target], seg_sem.at[7 + source],
+            2 * lax.div(right, 2) + target,
+        )
+
     seg_left = remote(seg_buf.at[0], seg_buf.at[2], seg_sem.at[5], seg_sem.at[6], left)
     pl.semaphore_wait(barrier, jnp.where(has_right, 3 - core, 1))
 
@@ -154,6 +160,8 @@
 
         @pl.when(has_right & (core == source))
         def _():
+            for target in range(2):
+                seg_right(source, target).start()
             for t in range(DELAY):
                 for target in range(2):
                     for i in range(2):
@@ -192,10 +200,6 @@
 
     seg_local.wait()
     seg_remote.wait_recv()
-
-    @pl.when(has_right)
-    def _():
-        seg_right.start()
 
     def rows(ref, h, at, blocks):
         parts = [ref[h, at + b : at + b + 1, :] for b in range(blocks)]
@@ -280,6 +284,37 @@
             jnp.concatenate(lse_in[:2], 1), jnp.concatenate(delta_in[:2], 1), ((s1, d1), (s2, d2))
         )
         lse_out, delta_out = [lse[:, :hd], lse[:, hd:]], [delta[:, :hd], delta[:, hd:]]
+        @pl.when(has_left)
+        def _():
+            dkl_sum = dvl_sum = None
+            dkl, dvl = dot_nn(e2, qa), dot_nn(p2, ga)
+            stay_here = []
+            for b in range(2):
+                at = slice(b * wide, (b + 1) * wide)
+                q, g = q_all[at, col(h)], g_all[at, col(h)]
+                s = dot_nt(kl, q) * scale + b_left[:, at]
+                dp = dot_nt(vl, g)
+                lse, delta, ((p, e),) = merge(
+                    rows(st_own, h, 2 * b, 2), rows(st_own, h, 4 + 2 * b, 2), ((s, dp),)
+                )
+                put_rows(st_tot, h, 2 * b, lse)
+                put_rows(st_tot, h, 4 + 2 * b, delta)
+                stay_here.append((at, p, e))
+                dkb, dvb = dot_nn(e, q), dot_nn(p, g)
+                dkl_sum = dkb if b == 0 else dkl_sum + dkb
+                dvl_sum = dvb if b == 0 else dvl_sum + dvb
+            for i, (total, extra, kept) in enumerate(((dkl_sum, dkl, q_all), (dvl_sum, dvl, g_all))):
+                stay = kept[:span, col(nxt)].astype(F32)
+                sendm[h, i * span : i * span + cut] = jnp.where(queries_left[:cut], stay[:cut], total[:cut]).astype(BF16)
+                sendm[h, i * span + cut : (i + 1) * span] = jnp.where(
+                    queries_left[cut:], stay[cut:], total[cut:] + extra
+                ).astype(BF16)
+
+            to_left(h).start()
+            for at, p, e in stay_here:
+                acc_o[h, at] = dot_tn(p, vl)
+                acc_dq[h, at] = dot_tn(e, kl)
+
         for i, (a1, b1, a2, b2, kept) in enumerate(
             ((p1, v, p2, vl[cut:], k_all), (e1, k, e2, kl[cut:], v_all))
         ):
@@ -300,39 +335,14 @@
         def _():
             to_right(h).start()
 
-        dkl_sum = dvl_sum = None
-        dkl, dvl = dot_nn(e2, qa), dot_nn(p2, ga)
-        stay_here = []
-        for b in range(2):
-            at = slice(b * wide, (b + 1) * wide)
-            q, g = q_all[at, col(h)], g_all[at, col(h)]
-            s = dot_nt(kl, q) * scale + b_left[:, at]
-            dp = dot_nt(vl, g)
-            lse, delta, ((p, e),) = merge(
-                rows(st_own, h, 2 * b, 2), rows(st_own, h, 4 + 2 * b, 2), ((s, dp),)
-            )
-            put_rows(st_tot, h, 2 * b, lse)
-            put_rows(st_tot, h, 4 + 2 * b, delta)
-            stay_here.append((at, p, e))
-            dkb, dvb = dot_nn(e, q), dot_nn(p, g)
-            dkl_sum = dkb if b == 0 else dkl_sum + dkb
-            dvl_sum = dvb if b == 0 else dvl_sum + dvb
-        for i, (total, extra, kept) in enumerate(((dkl_sum, dkl, q_all), (dvl_sum, dvl, g_all))):
-            stay = kept[:span, col(nxt)].astype(F32)
-            sendm[h, i * span : i * span + cut] = jnp.where(queries_left[:cut], stay[:cut], total[:cut]).astype(BF16)
-            sendm[h, i * span + cut : (i + 1) * span] = jnp.where(
-                queries_left[cut:], stay[cut:], total[cut:] + extra
-            ).astype(BF16)
-
-        @pl.when(has_left)
-        def _():
-            to_left(h).start()
+        @pl.when(jnp.logical_not(has_left))
+        def _():
+            st_tot[h] = st_own[h]
+            acc_o[h] = jnp.zeros((own, hd), F32)
+            acc_dq[h] = jnp.zeros((own, hd), F32)
 
         acc_dk[h] = dot_nn(e1, qa) + dot_nn(e3, qb)
         acc_dv[h] = dot_nn(p1, ga) + dot_nn(p3, gb)
-        for at, p, e in stay_here:
-            acc_o[h, at] = dot_tn(p, vl)
-            acc_dq[h, at] = dot_tn(e, kl)
 
     def close(h):
         t = h + DELAY
@@ -405,17 +415,23 @@
         for j in range(4):
             in_local(j, t).wait()
             in_remote(j, t).wait_recv()
-        first[t] = own_stats(t)
+        if t == 0:
+            first[0] = own_stats(0)
+        else:
+
+            @pl.when(has_left)
+            def _():
+                first[t] = own_stats(t)
 
     @pl.when(has_left)
     def _():
         pl.semaphore_wait(ready.at[0], 1)
+        seg_left.start()
         for t in range(DELAY):
             for i in range(3):
                 early_left(t, i).start()
-            if t == 0:
-                seg_left.start()
-        seg_right.wait_recv()
+        for source in range(2):
+            seg_right(source, 0).wait_recv()
 
     @pl.when(has_right)
     def _():
@@ -446,7 +462,7 @@
                 in_local(j, DELAY).wait()
                 in_remote(j, DELAY).wait_recv()
 
-        @pl.when(i + DELAY < heads)
+        @pl.when((i + DELAY < heads) & has_left)
         def _():
             sendm[i, 2 * span :] = own_stats(i + DELAY)
 
@@ -482,6 +498,10 @@
         @pl.when(i < heads)
         def _():
             cross(i)
+
+        @pl.when((i < heads - 1) & jnp.logical_not(has_left))
+        def _():
+            own_stats(i + 1)
 
         @pl.when(i >= DELAY)
         def _():
@@ -518,7 +538,8 @@
 
     @pl.when(has_right)
     def _():
-        seg_right.wait_send()
+        for target in range(2):
+            seg_right(0, target).wait_send()
 
     @pl.when(has_left)
     def _():
@@ -561,7 +582,7 @@
             vm((heads, own, hd), F32), vm((heads, own, hd), F32),
             vm((heads, own, hd), F32), vm((heads, own, hd), F32),
             vm((heads, 4, own, hd), BF16),
-            dma((4, DELAY + 1)), dma((4, DELAY + 1)), dma((4, DELAY + 1)), dma((7,)),
+            dma((4, DELAY + 1)), dma((4, DELAY + 1)), dma((4, DELAY + 1)), dma((9,)),
             dma((DELAY, 2, 2)), dma((DELAY, 2, 2)), dma((DELAY, 3)), dma((DELAY, 3)),
             dma((2, heads)), dma((2, heads)), pltpu.SemaphoreType.REGULAR((2,)),
             dma((4, heads)), dma((4, heads)),

time: 70.4 us -> 70.3 us (level)
  no operation moved by 1% of the time
where the time goes in v5:
time: 70.3 us; the launch traced here: 70.1 us
  Pallas kernels  69.5 us (99%)
    pallas_call x1, Pallas kernels, local(): pl.pallas_call(functools.partial(kernel, n), out_shape=(vm((tok, feature)...  67.5 us
    pallas_call x1, Pallas kernels, local(): pl.pallas_call(store, out_shape=(out,) * 4, in_specs=[pl.BlockSpec(memory...  2.04 us

profile of v5, /device:TPU:37, one launch (start us, length us, event | category | flops | bytes accessed | tf_op | source)
XLA Modules:
  0.0 70.1 jit_solution(10431423556373861575)
XLA Ops:
  0.6 67.5 %packed_attention.1 = (bf16[256,2048]{1,0:T(8,128)(2,1)S(1)}, bf16[256,2048]{1,0:T(8,128)(2,1)S(1)}, bf16[256,2048]{1,0:T(8,128)(2,1)S(1)}, bf16[256,2048]{1,0:T(8,128)(2,1)S(1)}) custom-call(bf16[256,2048]{1,0:T(8,128)(2,1)} %q_h.1, bf16[256,2048]{1,0:T(8,128)(2,1)} %k_h.1, bf16[256,2048]{1,0:T(8,128)(2,1)} %v_h.1, bf16[256,2048]{1,0:T(8,128)(2,1)} %g_h.1, ...), custom_call_target="tpu_custom_call" | custom-call | tf_op jit(solution)/shard_map/packed_attention/pallas_call | solution.py:568
  68.1 2.0 %store_results.1 = (bf16[256,2048]{1,0:T(8,128)(2,1)}, bf16[256,2048]{1,0:T(8,128)(2,1)}, bf16[256,2048]{1,0:T(8,128)(2,1)}, bf16[256,2048]{1,0:T(8,128)(2,1)}) custom-call(bf16[256,2048]{1,0:T(8,128)(2,1)S(1)} %get-tuple-element.8.refs_0_, bf16[256,2048]{1,0:T(8,128)(2,1)S(1)} %get-tuple-element.9.refs_1_, bf16[256,2048]{1,0:T(8,128)(2,1)S(1)} %get-tuple-element.10.refs_2_, ...), custom_call_target="tpu_custom_call" | custom-call | tf_op jit(solution)/shard_map/store_results/pallas_call | solution.py:595
